TPU v7x, 32 devices: a whole 2x2x4 slice. The times are simulated.
32 devices in a mesh: rep: 2 (over x), fsdp: 4 (over z), ep: 4 (over y, core).
Axes of the slice: x: 2, y: 2, z: 4, core: 2. Of those that a mesh axis runs over, the one named last changes fastest.
Arguments:
- tokens: bfloat16 [32768, 1024], P(('rep', 'fsdp', 'ep')), parts along dimension 0
- expert_idx: int32 [32768, 8], P(('rep', 'fsdp', 'ep')), parts along dimension 0
- gates: float32 [32768, 8], P(('rep', 'fsdp', 'ep')), parts along dimension 0
- w_gate: bfloat16 [32, 1024, 512], P('ep', 'fsdp')
- w_up: bfloat16 [32, 1024, 512], P('ep', 'fsdp')
- w_down: bfloat16 [32, 512, 1024], P('ep', None, 'fsdp')
Outputs:
- output: bfloat16 [32768, 1024], P(('rep', 'fsdp', 'ep')), parts along dimension 0
There are 2 independent parts. A program takes and returns all parts, laid end to end along the dimension named above; an argument that names none is the same for every part.
All inputs are finite; a program needn't handle non-finite values.
Results may differ from a plain program's by a relative error of at most 0.001.
Values are sent between devices in bfloat16 or wider.
A program may use at most 1 GiB of HBM per device.

v0:
```python
import jax
import jax.numpy as jnp
from jax import lax
from jax.sharding import PartitionSpec as P


def slot_plan(flat_ids, n_experts, capacity, n_choice):
    n_pairs = flat_ids.shape[0]
    pair_order = jnp.argsort(flat_ids, stable=True)
    sorted_ids = flat_ids[pair_order]
    expert_range = jnp.arange(n_experts, dtype=flat_ids.dtype)
    first_pos = jnp.searchsorted(sorted_ids, expert_range, side='left')
    last_pos = jnp.searchsorted(sorted_ids, expert_range, side='right')
    slot_pos = first_pos[:, None] + jnp.arange(capacity)[None, :]
    pair_at = pair_order[jnp.minimum(slot_pos, n_pairs - 1)]
    source_row = jnp.where(slot_pos < last_pos[:, None], pair_at // n_choice, n_pairs // n_choice)
    rank_of_pair = jnp.argsort(pair_order)
    pair_slot = flat_ids * capacity + rank_of_pair - first_pos[flat_ids]
    return source_row.reshape(-1), pair_slot


def solution(mesh):
    ep_size = mesh.shape['ep']
    tok_spec = P(('rep', 'fsdp', 'ep'), None)

    def device_step(x_blk, ids_blk, gate_blk, wg_blk, wu_blk, wd_blk):
        tok_per_dev, d_model = x_blk.shape
        n_choice = ids_blk.shape[1]
        local_experts = wg_blk.shape[0]
        n_experts = local_experts * ep_size
        capacity = min(tok_per_dev // 2, 4 * n_choice * tok_per_dev // n_experts)
        source_row, pair_slot = slot_plan(ids_blk.reshape(-1), n_experts, capacity, n_choice)
        send_buf = jnp.take(x_blk, source_row, axis=0, mode='fill', fill_value=0)
        send_buf = send_buf.reshape(ep_size, local_experts, capacity, d_model)
        recv_rows = lax.all_to_all(send_buf, 'ep', 0, 2, tiled=True)
        recv_rows = recv_rows.reshape(local_experts, ep_size * capacity, d_model)
        full_wg = lax.all_gather(wg_blk, 'fsdp', axis=1, tiled=True)
        full_wu = lax.all_gather(wu_blk, 'fsdp', axis=1, tiled=True)
        full_wd = lax.all_gather(wd_blk, 'fsdp', axis=2, tiled=True)
        act_g = jnp.einsum('nrd,ndf->nrf', recv_rows, full_wg, preferred_element_type=jnp.float32)
        act_u = jnp.einsum('nrd,ndf->nrf', recv_rows, full_wu, preferred_element_type=jnp.float32)
        hidden = (jax.nn.silu(act_g) * act_u).astype(jnp.bfloat16)
        expert_out = jnp.einsum('nrf,nfd->nrd', hidden, full_wd,
                                preferred_element_type=jnp.float32).astype(jnp.bfloat16)
        expert_out = expert_out.reshape(1, local_experts, ep_size * capacity, d_model)
        returned = lax.all_to_all(expert_out, 'ep', 2, 0, tiled=True)
        returned = returned.reshape(n_experts * capacity, d_model)
        picked = jnp.take(returned, pair_slot, axis=0).reshape(tok_per_dev, n_choice, d_model)
        mixed = jnp.sum(gate_blk[:, :, None] * picked.astype(jnp.float32), axis=1)
        return (x_blk.astype(jnp.float32) + mixed).astype(jnp.bfloat16)

    return jax.shard_map(
        device_step, mesh=mesh,
        in_specs=(tok_spec, tok_spec, tok_spec, P('ep', 'fsdp', None), P('ep', 'fsdp', None), P('ep', None, 'fsdp')),
        out_specs=tok_spec, check_vma=False)
```

profile of v0, /device:TPU:1, one launch (start us, length us, event | category | flops | bytes accessed | tf_op | source)
XLA Modules:
  0.0 1357.0 jit_solution(5088071934942968110)
XLA Ops:
  6.5 0.7 all-gather.4.cloned.1.call-update
  7.3 1.0 copy.19
  8.3 0.3 reshape.246
  8.5 6.8 sort.34
  15.3 45.5 %gather_fusion.2 = s32[8192]{0:T(1024)S(1)} fusion(s32[8192]{0:T(1024)S(1)} %reshape.246, s32[8192]{0:T(1024)S(1)} %fusion.13), kind=kCustom, calls=%fused_computation.2 | custom fusion | bytes 98304 | tf_op jit(solution)/shard_map/gather | solution.py:10
  60.9 10.5 while.48
  60.9 0.7 gather_fusion
  61.6 0.7 gather_fusion
  62.4 0.7 gather_fusion
  63.2 0.7 gather_fusion
  63.9 0.7 gather_fusion
  64.7 0.7 gather_fusion
  65.4 0.7 gather_fusion
  66.2 0.7 gather_fusion
  66.9 0.7 gather_fusion
  67.7 0.7 gather_fusion
  68.4 0.7 gather_fusion
  69.2 0.7 gather_fusion
  69.9 0.7 gather_fusion
  70.7 0.7 gather_fusion
  71.6 10.5 while.49
  71.6 0.7 gather_fusion.1
  72.4 0.7 gather_fusion.1
  73.1 0.7 gather_fusion.1
  73.9 0.7 gather_fusion.1
  74.6 0.7 gather_fusion.1
  75.4 0.7 gather_fusion.1
  76.1 0.7 gather_fusion.1
  76.9 0.7 gather_fusion.1
  77.6 0.7 gather_fusion.1
  78.4 0.7 gather_fusion.1
  79.1 0.7 gather_fusion.1
  79.9 0.7 gather_fusion.1
  80.6 0.7 gather_fusion.1
  81.4 0.7 gather_fusion.1
  82.4 90.5 %gather_fusion.3 = s32[16384]{0:T(1024)S(1)} fusion(s32[8192]{0:T(1024)S(1)} %get-tuple-element.137, s32[16384]{0:T(1024)S(1)} %broadcast_clamp_fusion.1), kind=kCustom, calls=%fused_computation.3 | custom fusion | bytes 196608 | tf_op jit(solution)/shard_map/gather | solution.py:15
  173.0 0.4 compare_select_fusion
  173.4 69.7 %gather_fusion.4 = bf16[16384,1024]{1,0:T(8,128)(2,1)} fusion(bf16[1024,1024]{1,0:T(8,128)(2,1)S(1)} %copy-done.2, s32[16384]{0:T(1024)S(1)} %broadcast_clamp_fusion), kind=kCustom, calls=%fused_computation.4 | custom fusion | bytes 67174400 | tf_op jit(solution)/shard_map/jit(_take)/gather | solution.py:33
  243.2 0.1 compare_and_fusion
  243.3 22.8 %broadcast_select_fusion.4 = bf16[4,8,512,1024]{3,2,1,0:T(8,128)(2,1)} fusion(bf16[4,8,512,1024]{3,2,1,0:T(8,128)(2,1)} %bitcast.71, pred[4,8,512]{2,1,0:T(8,128)(4,1)S(1)} %compare_and_fusion), kind=kLoop, calls=%fused_computation.25 | loop fusion | flops 16777216 | bytes 67125248 | tf_op jit(solution)/shard_map/jit(_take)/select_n | solution.py:33
  266.1 9.7 all-to-all-start
  275.8 0.7 all-gather.6.cloned.1.call-update
  276.5 0.2 all-gather.8.cloned.1.call-start
  276.7 0.5 all-gather.8.cloned.1.call-update
  277.2 360.6 %all-to-all-done = bf16[4,8,512,1024]{3,2,1,0:T(8,128)(2,1)} async-done(((bf16[4,8,512,1024]{3,2,1,0:T(8,128)(2,1)}), bf16[4,8,512,1024]{3,2,1,0:T(8,128)(2,1)}, u32[]{:S(2)}, u32[]{:S(2)}) %all-to-all-start) | async-done | bytes 33554464 | tf_op jit(solution)/shard_map/all_to_all | solution.py:35
  637.8 22.6 %copy.21 = bf16[1,8,4,512,1024]{4,3,2,1,0:T(8,128)(2,1)} copy(bf16[1,8,4,512,1024]{4,3,1,2,0:T(8,128)(2,1)} %bitcast.37) | data formatting | bytes 67108864 | tf_op jit(solution)/shard_map/all_to_all | solution.py:35
  660.4 33.7 %fusion.17 = f32[8,2048,512]{2,1,0:T(8,128)} fusion(bf16[8,2048,1024]{2,1,0:T(8,128)(2,1)} %bitcast.72, bf16[8,1024,512]{2,1,0:T(8,128)(2,1)} %all-gather.4.cloned.1.call-done), kind=kOutput, calls=%fused_computation.91 | convolution fusion | flops 17179869184 | bytes 75497472 | tf_op jit(solution)/shard_map/nrd,ndf->nrf/dot_general | solution.py:40
  694.2 52.1 %convert_bitcast_fusion = bf16[1,8,2048,1024]{3,2,1,0:T(8,128)(2,1)} fusion(bf16[8,512,1024]{2,1,0:T(8,128)(2,1)} %all-gather.8.cloned.1.call-done, f32[8,2048,512]{2,1,0:T(8,128)} %fusion.17, bf16[8,2048,1024]{2,1,0:T(8,128)(2,1)} %bitcast.73, bf16[8,1024,512]{2,1,0:T(8,128)(2,1)} %all-gather.6.cloned.1.call-done), kind=kOutput, calls=%fused_computation.23 | convolution fusion | flops 34426847232 | bytes 117440512 | tf_op jit(solution)/shard_map/nrf,nfd->nrd/dot_general | solution.py:43
  746.3 30.8 %copy.22 = bf16[1,8,2048,1024]{3,1,0,2:T(8,128)(2,1)} copy(bf16[1,8,2048,1024]{3,2,1,0:T(8,128)(2,1)} %convert_bitcast_fusion) | data formatting | bytes 67108864 | tf_op jit(solution)/shard_map/reshape | solution.py:45
  777.1 11.0 all-to-all-start.1
  788.1 0.3 reshape.247
  788.4 6.8 sort.35
  795.2 0.7 fusion.16
  795.9 0.7 fusion.15
  796.6 4.5 compare_select_fusion.7
  801.1 2.5 compare_reduce_fusion.24
  803.6 15.7 %compare_and_fusion.1 = (pred[8192]{0:T(1024)(128)(4,1)S(1)}, s32[8192]{0:T(1024)S(1)}) fusion(pred[8192]{0:T(1024)(128)(4,1)S(1)} %get-tuple-element.199, pred[8192]{0:T(1024)(128)(4,1)S(1)} %get-tuple-element.198, pred[8192]{0:T(1024)(128)(4,1)S(1)} %get-tuple-element.197, pred[8192]{0:T(1024)(128)(4,1)S(1)} %get-tuple-element.196, ...), kind=kLoop, calls=%fused_computation.86 | loop fusion | flops 278528 | bytes 344164 | tf_op jit(solution)/shard_map/jit(_take)/and | solution.py:48
  819.4 0.3 broadcast_in_dim.74
  819.7 0.2 copy.18
  819.9 329.8 %all-to-all-done.1 = bf16[1,8,2048,1024]{3,1,0,2:T(8,128)(2,1)} async-done(((bf16[1,8,2048,1024]{3,1,0,2:T(8,128)(2,1)}), bf16[1,8,2048,1024]{3,1,0,2:T(8,128)(2,1)}, u32[]{:S(2)}, u32[]{:S(2)}) %all-to-all-start.1) | async-done | bytes 33554464 | tf_op jit(solution)/shard_map/all_to_all | solution.py:46
  1149.7 30.8 %copy.23 = bf16[1,8,4,512,1024]{4,3,1,2,0:T(8,128)(2,1)} copy(bf16[1,8,4,512,1024]{4,1,3,2,0:T(8,128)(2,1)} %bitcast.40) | data formatting | bytes 67108864 | tf_op jit(solution)/shard_map/all_to_all | solution.py:46
  1180.5 150.7 %gather_fusion.5 = bf16[8192,1024]{1,0:T(8,128)(2,1)} fusion(bf16[16384,1024]{1,0:T(8,128)(2,1)} %bitcast.70, s32[8192]{0:T(1024)S(1)} %broadcast_clamp_fusion.2), kind=kCustom, calls=%fused_computation.5 | custom fusion | bytes 33587200 | tf_op jit(solution)/shard_map/jit(_take)/gather | solution.py:48
  1331.3 16.9 %multiply_reduce_fusion = f32[1024,1024]{1,0:T(8,128)S(1)} fusion(bf16[8192,1024]{1,0:T(8,128)(2,1)} %gather_fusion.5, f32[1024,8]{1,0:T(8,128)S(1)} %copy.18, pred[1024,8]{1,0:T(8,128)(4,1)S(1)} %broadcast_in_dim.74), kind=kLoop, calls=%fused_computation.22 | loop fusion | flops 32505856 | bytes 21012480 | tf_op jit(solution)/shard_map/reduce_sum | solution.py:49
  1348.2 2.2 add_convert_fusion
  (130 shorter events, 1.4 us)
Async XLA Ops:
  6.5 653.9 %all-gather.4.cloned.1.call-start = ((), (), s32[]{:S(2)}) async-start(), calls=%async_computation.2 | async-start | bytes 10485760 | tf_op jit(solution)/shard_map/all_gather | solution.py:37
  8.3 7.0 copy-start.6
  8.5 73.8 %copy-start.4 = (s32[8192]{0:T(1024)}, s32[8192]{0:T(1024)S(1)}, u32[]{:S(2)}) copy-start(s32[8192]{0:T(1024)S(1)} %reshape.246) | copy-start | bytes 98308
  15.3 157.7 %copy-start = (s32[8192]{0:T(1024)}, s32[8192]{0:T(1024)S(1)}, u32[]{:S(2)}) copy-start(s32[8192]{0:T(1024)S(1)} %get-tuple-element.137) | copy-start | bytes 98308
  71.4 10.9 copy-start.8
  82.4 91.0 %copy-start.2 = (bf16[1024,1024]{1,0:T(8,128)(2,1)S(1)}, bf16[1024,1024]{1,0:T(8,128)(2,1)}, u32[]{:S(2)}) copy-start(bf16[1024,1024]{1,0:T(8,128)(2,1)} %param.10) | copy-start | bytes 6291460
  266.1 371.7 %all-to-all-start = ((bf16[4,8,512,1024]{3,2,1,0:T(8,128)(2,1)}), bf16[4,8,512,1024]{3,2,1,0:T(8,128)(2,1)}, u32[]{:S(2)}, u32[]{:S(2)}) async-start(bf16[4,8,512,1024]{3,2,1,0:T(8,128)(2,1)} %broadcast_select_fusion.4), calls=%async_computation | async-start | bytes 67108864 | tf_op jit(solution)/shard_map/all_to_all | solution.py:35
  275.7 418.4 %all-gather.6.cloned.1.call-start = ((), (), s32[]{:S(2)}) async-start(), calls=%async_computation.3 | async-start | bytes 10485760 | tf_op jit(solution)/shard_map/all_gather | solution.py:38
  276.5 417.7 %all-gather.8.cloned.1.call-start = ((), (), s32[]{:S(2)}) async-start(), calls=%async_computation.4 | async-start | bytes 10485760 | tf_op jit(solution)/shard_map/all_gather | solution.py:39
  777.0 11.0 copy-start.7
  777.0 11.3 copy-start.1
  777.1 18.1 %copy-start.9 = (s32[32]{0:T(128)S(1)}, s32[32]{0:T(128)}, u32[]{:S(2)}) copy-start(s32[32]{0:T(128)} %copy-done.8) | copy-start | bytes 388
  777.1 26.6 %copy-start.5 = (s32[8192]{0:T(1024)S(1)}, s32[8192]{0:T(1024)}, u32[]{:S(2)}) copy-start(s32[8192]{0:T(1024)} %copy-done.4) | copy-start | bytes 98308
  777.1 42.6 %copy-start.10 = (f32[1024,8]{0,1:T(8,128)S(1)}, f32[1024,8]{0,1:T(8,128)}, u32[]{:S(2)}) copy-start(f32[1024,8]{0,1:T(8,128)} %param.12) | copy-start | bytes 98308
  777.1 372.6 %all-to-all-start.1 = ((bf16[1,8,2048,1024]{3,1,0,2:T(8,128)(2,1)}), bf16[1,8,2048,1024]{3,1,0,2:T(8,128)(2,1)}, u32[]{:S(2)}, u32[]{:S(2)}) async-start(bf16[1,8,2048,1024]{3,1,0,2:T(8,128)(2,1)} %copy.22), calls=%async_computation.1 | async-start | bytes 67108864 | tf_op jit(solution)/shard_map/all_to_all | solution.py:46
  1180.5 167.7 %copy-start.3 = (bf16[1024,1024]{1,0:T(8,128)(2,1)S(1)}, bf16[1024,1024]{1,0:T(8,128)(2,1)}, u32[]{:S(2)}) copy-start(bf16[1024,1024]{1,0:T(8,128)(2,1)} %param.10) | copy-start | bytes 6291460
Sparse Core Ops, SparseCore 0:
  8.9 151.6 all-gather.3
  278.1 152.1 all-gather.5
  431.9 148.4 all-gather.7
where the time goes:
time: 1360 us
  waiting for transfers between devices  692 us (51%)
  local copies, waits for them, and re-layouts  464 us (34%)
  matrix products  85.9 us (6%)
  other arithmetic  79.7 us (6%)
  starting transfers between devices  20.9 us (2%)
    all_to_all x1, waiting for transfers between devices, device_step(): recv_rows = lax.all_to_all(send_buf, 'ep', 0, 2, tiled=True)  361 us
    all_to_all x1, waiting for transfers between devices, device_step(): returned = lax.all_to_all(expert_out, 'ep', 2, 0, tiled=True)  330 us
    gather x1, local copies, waits for them, and re-layouts, device_step(): jnp.take(returned, pair_slot, axis=0)  151 us
    gather x2, local copies, waits for them, and re-layouts, slot_plan(): pair_at = pair_order[jnp.minimum(slot_pos, n_pairs - 1)]  90.5 us
    gather x1, local copies, waits for them, and re-layouts, device_step(): send_buf = jnp.take(x_blk, source_row, axis=0, mode='fill', fill_value=0)  69.7 us
    dot_general x1, matrix products, device_step(): jnp.einsum('nrf,nfd->nrd', hidden, full_wd, preferred_element_type=jnp.fl...  52.1 us
    gather x1, local copies, waits for them, and re-layouts, slot_plan(): sorted_ids = flat_ids[pair_order]  45.5 us
    dot_general x1, matrix products, device_step(): jnp.einsum('nrd,ndf->nrf', recv_rows, full_wg, preferred_element_type=jnp...  33.7 us
  transfers between devices with their start and end apart: 5, of which 2 were waited for; matrix products, arithmetic and copies ran while one was open for 26% of the time, Pallas kernels for 0%

commit v1 on v0

v1 whole, which is shorter than its diff:
```python
import functools

import jax
import jax.numpy as jnp
from jax import lax
from jax.experimental import pallas as pl
from jax.experimental.pallas import tpu as pltpu
from jax.sharding import PartitionSpec as P

MESH = pl.DeviceIdType.MESH
N_Z = 4
N_BLOCK = 2


def moe_kernel(x_hbm, ids_hbm, gates_hbm, wg_hbm, wu_hbm, wd_hbm, out_hbm,
               wg, wu, wd, toks, ids, gates, acc, from_core, from_y,
               own_sem, recv_z, recv_x, send_r, send_l, send_x,
               tok_send, tok_recv, meta_send, meta_recv,
               sum_send, sum_recv, credit, out_sem):
    r = lax.axis_index('rep')
    z = lax.axis_index('fsdp')
    p = lax.axis_index('ep')
    core = p % 2
    core_peer = p + 1 - 2 * core
    y_peer = (p + 2) % 4
    far_peer = (core_peer + 2) % 4
    n_local = wg_hbm.shape[0]
    n_packet = n_local // 2
    d_shard = wg_hbm.shape[1]
    n_tok = x_hbm.shape[0]
    block = n_tok // N_BLOCK

    hbm = (wg_hbm, wu_hbm, wd_hbm)

    def shard(t, e, s):
        start = pl.multiple_of(s * d_shard, d_shard)
        if t == 2:
            return wd.at[e, :, pl.ds(start, d_shard)]
        return (wg, wu)[t].at[e, pl.ds(start, d_shard), :]

    def remote(src, dst, send_sem, recv_sem, **where):
        return pltpu.make_async_remote_copy(src_ref=src, dst_ref=dst, send_sem=send_sem, recv_sem=recv_sem,
                                            device_id=where, device_id_type=MESH)

    def z_copy(t, k, s, right, own):
        e = 2 * k + r
        src = hbm[t].at[e] if own else shard(t, e, s)
        send = send_r if right else send_l
        to = (z + 1) % N_Z if right else (z + N_Z - 1) % N_Z
        return remote(src, shard(t, e, s), send.at[t, k, s], recv_z.at[t, k, s], fsdp=to)

    def x_copy(t, k, s):
        e = 2 * k + r
        return remote(shard(t, e, s), shard(t, e, s), send_x.at[t, k, s], recv_x.at[t, k, s], rep=1 - r)

    def x_arrival(t, k, s):
        e = 2 * k + 1 - r
        return remote(shard(t, e, s), shard(t, e, s), send_x.at[t, k, s], recv_x.at[t, k, s], rep=1 - r)

    def send_own(k):
        for t in range(3):
            @pl.when(z > 0)
            def _():
                z_copy(t, k, z, False, True).start()

            @pl.when(z < N_Z - 1)
            def _():
                z_copy(t, k, z, True, True).start()

    def event(k, dist, t):
        left = (z + N_Z - dist) % N_Z
        right = (z + dist) % N_Z

        @pl.when(z + dist < N_Z)
        def _():
            z_copy(t, k, right, False, False).wait_recv()

            @pl.when(z > 0)
            def _():
                z_copy(t, k, right, False, False).start()
            x_copy(t, k, right).start()

        @pl.when(z >= dist)
        def _():
            z_copy(t, k, left, True, False).wait_recv()

            @pl.when(z < N_Z - 1)
            def _():
                z_copy(t, k, left, True, False).start()
            x_copy(t, k, left).start()

    def wait_x(k):
        for dist in range(1, N_Z):
            for t in range(3):
                x_arrival(t, k, (z + dist) % N_Z).wait_recv()

    barrier = pltpu.get_barrier_semaphore()
    for peer in (core_peer, y_peer, far_peer):
        pl.semaphore_signal(barrier, inc=1, device_id={'ep': peer}, device_id_type=MESH)
    pl.semaphore_signal(barrier, inc=1, device_id={'rep': 1 - r}, device_id_type=MESH)

    @pl.when(z > 0)
    def _():
        pl.semaphore_signal(barrier, inc=1, device_id={'fsdp': (z + N_Z - 1) % N_Z}, device_id_type=MESH)

    @pl.when(z < N_Z - 1)
    def _():
        pl.semaphore_signal(barrier, inc=1, device_id={'fsdp': (z + 1) % N_Z}, device_id_type=MESH)

    own_w = [pltpu.make_async_copy(hbm[t].at[e], shard(t, e, z), own_sem.at[t, e])
             for e in range(n_local) for t in range(3)]
    own_x = pltpu.make_async_copy(x_hbm, toks.at[3], own_sem.at[3, 0])
    own_ids = pltpu.make_async_copy(ids_hbm, ids.at[3], own_sem.at[3, 1])
    own_gates = pltpu.make_async_copy(gates_hbm, gates.at[3], own_sem.at[3, 2])
    own_copies = own_w + [own_x, own_ids, own_gates]
    for copy in own_copies:
        copy.start()

    pl.semaphore_wait(barrier, 4 + (z + N_Z - 1) // N_Z + (2 * N_Z - 2 - z) // N_Z)

    meta = []
    for slot, peer in ((2, core_peer), (1, y_peer), (0, far_peer)):
        meta.append(remote(ids_hbm, ids.at[slot], meta_send.at[0, slot], meta_recv.at[0, slot], ep=peer))
        meta.append(remote(gates_hbm, gates.at[slot], meta_send.at[1, slot], meta_recv.at[1, slot], ep=peer))
    for copy in meta:
        copy.start()
    send_own(0)
    tok_core = remote(x_hbm, toks.at[2], tok_send.at[2], tok_recv.at[2], ep=core_peer)
    tok_y = remote(x_hbm, toks.at[1], tok_send.at[1], tok_recv.at[1], ep=y_peer)
    tok_far = remote(toks.at[1], toks.at[0], tok_send.at[0], tok_recv.at[0], ep=core_peer)
    tok_core.start()
    tok_y.start()
    send_own(1)

    def zero(i, carry):
        rows = pl.ds(pl.multiple_of(i % N_BLOCK * block, block), block)
        acc[i // N_BLOCK, rows, :] = jnp.zeros((block, acc.shape[2]), jnp.float32)
        return carry

    lax.fori_loop(0, 4 * N_BLOCK, zero, 0)

    for dist in range(1, N_Z):
        for t in range(3):
            event(0, dist, t)
    for copy in own_copies:
        copy.wait()
    tok_y.wait_recv()
    tok_far.start()
    for copy in meta:
        copy.wait_recv()
    tok_core.wait_recv()
    wait_x(0)
    tok_far.wait_recv()

    def place(i):
        far = i < 2 * N_BLOCK
        slot = jnp.where(far, i % 2, i // N_BLOCK)
        row = jnp.where(far, i // 2, i % N_BLOCK)
        return slot, row

    def compute(e, slot, row):
        rows = pl.ds(pl.multiple_of(row * block, block), block)
        x = toks[slot, rows, :]
        a = jnp.dot(x, wg[e], preferred_element_type=jnp.float32)
        b = jnp.dot(x, wu[e], preferred_element_type=jnp.float32)
        h = (a * jax.nn.sigmoid(a) * b).astype(jnp.bfloat16)
        o = jnp.dot(h, wd[e], preferred_element_type=jnp.float32).astype(jnp.bfloat16).astype(jnp.float32)
        expert = p * n_local + e
        chosen = jnp.where(ids[slot, :, rows] == expert, gates[slot, :, rows], 0.0)
        gate = jnp.sum(chosen, axis=0, keepdims=True)
        gate = jnp.broadcast_to(gate, (128, block)).T
        for c in range(acc.shape[2] // 128):
            cols = slice(c * 128, (c + 1) * 128)
            acc[slot, rows, cols] += jnp.where(gate > 0, gate * o[:, cols], 0.0)

    n_step = 4 * N_BLOCK * 2

    def packet(k, carry):
        @pl.when(k + 2 < n_packet)
        def _():
            send_own(k + 2)

        def step(i, carry):
            for j in range(9):
                @pl.when(i == j * n_step // 9)
                def _():
                    event(k + 1, j // 3 + 1, j % 3)
            slot, row = place(i // 2)
            compute(2 * k + i % 2, slot, row)
            return carry

        lax.fori_loop(0, n_step, step, 0)
        wait_x(k + 1)
        return carry

    lax.fori_loop(0, n_packet - 1, packet, 0)

    def block_of(ref, row):
        return ref.at[pl.ds(row * block, block), :]

    def to_core(slot, row):
        return remote(block_of(acc.at[slot], row), block_of(from_core, row),
                      sum_send.at[slot, row], sum_recv.at[slot, row], ep=core_peer)

    def to_y(row):
        return remote(block_of(acc.at[1], row), block_of(from_y, row),
                      sum_send.at[1, row], sum_recv.at[1, row], ep=y_peer)

    def last_step(i, carry):
        slot, row = place(i // 2)
        compute(2 * (n_packet - 1) + i % 2, slot, row)
        for n in range(N_BLOCK):
            @pl.when(i == 4 * n + 1)
            def _():
                to_core(0, n).start()

            @pl.when(i == 4 * n + 3)
            def _():
                to_core(0, n).wait_recv()
                rows = slice(n * block, (n + 1) * block)
                acc[1, rows, :] += from_core[rows, :]
                to_y(n).start()
                pl.semaphore_signal(credit.at[n], inc=1, device_id={'ep': core_peer}, device_id_type=MESH)

            @pl.when(i == 4 * N_BLOCK + 2 * n + 1)
            def _():
                pl.semaphore_wait(credit.at[n], 1)
                to_core(2, n).start()
        return carry

    lax.fori_loop(0, n_step, last_step, 0)

    outs = []
    for n in range(N_BLOCK):
        rows = slice(n * block, (n + 1) * block)
        to_core(2, n).wait_recv()
        to_y(n).wait_recv()
        y = toks[3, rows, :].astype(jnp.float32) + (acc[3, rows, :] + from_core[rows, :] + from_y[rows, :])
        toks[3, rows, :] = y.astype(jnp.bfloat16)
        copy = pltpu.make_async_copy(block_of(toks.at[3], n), block_of(out_hbm, n), out_sem.at[n])
        copy.start()
        outs.append(copy)

    for copy in meta + [tok_core, tok_y, tok_far]:
        copy.wait_send()
    for n in range(N_BLOCK):
        to_core(0, n).wait_send()
        to_y(n).wait_send()
        to_core(2, n).wait_send()

    def drain(k, carry):
        for t in range(3):
            @pl.when(z > 0)
            def _():
                z_copy(t, k, z, False, True).wait_send()

            @pl.when(z < N_Z - 1)
            def _():
                z_copy(t, k, z, True, True).wait_send()
            for dist in range(1, N_Z):
                left = (z + N_Z - dist) % N_Z
                right = (z + dist) % N_Z

                @pl.when((z + dist < N_Z) & (z > 0))
                def _():
                    z_copy(t, k, right, False, False).wait_send()

                @pl.when((z >= dist) & (z < N_Z - 1))
                def _():
                    z_copy(t, k, left, True, False).wait_send()
                x_copy(t, k, (z + dist) % N_Z).wait_send()
        return carry

    lax.fori_loop(0, n_packet, drain, 0)
    for copy in outs:
        copy.wait()


def solution(mesh):
    tok_spec = P(('rep', 'fsdp', 'ep'), None)

    def device_step(x_blk, ids_blk, gate_blk, wg_blk, wu_blk, wd_blk):
        n_tok, d_model = x_blk.shape
        n_choice = ids_blk.shape[1]
        n_local, d_shard, ffn = wg_blk.shape
        dma = pltpu.SemaphoreType.DMA
        n_packet = n_local // 2
        any_space = pl.BlockSpec(memory_space=pl.ANY)
        flops = 4 * n_tok * n_local * 6 * d_model * ffn
        return pl.pallas_call(
            moe_kernel,
            out_shape=jax.ShapeDtypeStruct((n_tok, d_model), jnp.bfloat16),
            in_specs=[any_space] * 6,
            out_specs=any_space,
            scratch_shapes=[
                pltpu.VMEM((n_local, d_model, ffn), jnp.bfloat16),
                pltpu.VMEM((n_local, d_model, ffn), jnp.bfloat16),
                pltpu.VMEM((n_local, ffn, d_model), jnp.bfloat16),
                pltpu.VMEM((4, n_tok, d_model), jnp.bfloat16),
                pltpu.VMEM((4, n_choice, n_tok), jnp.int32),
                pltpu.VMEM((4, n_choice, n_tok), jnp.float32),
                pltpu.VMEM((4, n_tok, d_model), jnp.float32),
                pltpu.VMEM((n_tok, d_model), jnp.float32),
                pltpu.VMEM((n_tok, d_model), jnp.float32),
                dma((4, n_local)),
                dma((3, n_packet, N_Z)),
                dma((3, n_packet, N_Z)),
                dma((3, n_packet, N_Z)),
                dma((3, n_packet, N_Z)),
                dma((3, n_packet, N_Z)),
                dma((3,)),
                dma((3,)),
                dma((2, 3)),
                dma((2, 3)),
                dma((3, N_BLOCK)),
                dma((3, N_BLOCK)),
                pltpu.SemaphoreType.REGULAR((N_BLOCK,)),
                dma((N_BLOCK,)),
            ],
            compiler_params=pltpu.CompilerParams(
                collective_id=0, has_side_effects=True, vmem_limit_bytes=67043328),
            cost_estimate=pl.CostEstimate(flops=flops, bytes_accessed=32 << 20, transcendentals=0),
            name='moe',
        )(x_blk, ids_blk.T, gate_blk.T, wg_blk, wu_blk, wd_blk)

    return jax.shard_map(
        device_step, mesh=mesh,
        in_specs=(tok_spec, tok_spec, tok_spec, P('ep', 'fsdp', None), P('ep', 'fsdp', None), P('ep', None, 'fsdp')),
        out_specs=tok_spec, check_vma=False)
```

time: 1360 us -> 340 us (0.25)
  waiting for transfers between devices: 692 us -> 0 us
  local copies, waits for them, and re-layouts: 464 us -> 3.08 us
  Pallas kernels: 0 us -> 336 us
  matrix products: 85.9 us -> 0 us
  other arithmetic: 79.7 us -> 0 us
  starting transfers between devices: 20.9 us -> 0 us
    all_to_all x2 -> x0, waiting for transfers between devices: 690 us -> none  [the longest x1 361 us: device_step(): recv_rows = lax.all_to_all(send_buf, 'ep', 0, 2, tiled=True)]
    gather x35 -> x0, local copies, waits for them, and re-layouts: 378 us -> none  [the longest x1 151 us: device_step(): jnp.take(returned, pair_slot, axis=0)]
    pallas_call x0 -> x1, Pallas kernels: none -> 336 us  [device_step(): pl.pallas_call(moe_kernel, out_shape=jax.ShapeDtypeStruct((n_tok, d_model...]
    dot_general x2 -> x0, matrix products: 85.9 us -> none  [the longest x1 52.1 us: device_step(): jnp.einsum('nrf,nfd->nrd', hidden, full_wd, preferred_element_type=jnp.fl...]
    all_to_all x2 -> x0, local copies, waits for them, and re-layouts: 53.4 us -> none  [the longest x1 30.8 us: device_step(): returned = lax.all_to_all(expert_out, 'ep', 2, 0, tiled=True)]
    reshape x3 -> x0, local copies, waits for them, and re-layouts: 31.3 us -> none  [the longest x1 30.8 us: device_step(): expert_out.reshape(1, local_experts, ep_size * capacity, d_model)]
    select_n x30 -> x0, other arithmetic: 23.6 us -> none  [the longest x2 23.2 us: device_step(): send_buf = jnp.take(x_blk, source_row, axis=0, mode='fill', fill_value=0)]
    all_to_all x2 -> x0, starting transfers between devices: 20.7 us -> none  [the longest x1 11 us: device_step(): returned = lax.all_to_all(expert_out, 'ep', 2, 0, tiled=True)]
  transfers between devices with their start and end apart: 5 -> 0, of which waited for: 2 -> 0; matrix products, arithmetic and copies ran while one was open for 26% -> 0% of each run, Pallas kernels for 0% -> 0%
where the time goes in v1:
time: 340 us; the launch traced here: 339 us
  Pallas kernels  336 us (99%)
    pallas_call x1, Pallas kernels, device_step(): pl.pallas_call(moe_kernel, out_shape=jax.ShapeDtypeStruct((n_tok, d_model...  336 us

profile of v1, /device:TPU:1, one launch (start us, length us, event | category | flops | bytes accessed | tf_op | source)
XLA Modules:
  0.0 338.8 jit_solution(11975589720845340416)
XLA Ops:
  0.0 335.7 %moe.1 = bf16[1024,1024]{1,0:T(8,128)(2,1)} custom-call(bf16[1024,1024]{1,0:T(8,128)(2,1)} %x_hbm.1, s32[8,1024]{1,0:T(8,128)} %bitcast.2, f32[8,1024]{1,0:T(8,128)} %bitcast.3, bf16[8,256,512]{2,1,0:T(8,128)(2,1)} %wg_hbm.1, bf16[8,256,512]{2,1,0:T(8,128)(2,1)} %wu_hbm.1, bf16[8,512,256]{2,1,0:T(8,128)(2,1)} %wd_hbm.1), custom_call_target="tpu_custom_call" | custom-call | flops 103079215104 | bytes 33554432 | tf_op jit(solution)/shard_map/moe/pallas_call | solution.py:290
  335.7 3.1 copy.8

commit v2 on v1

--- a/solution.py
+++ b/solution.py
@@ -10,6 +10,7 @@
 MESH = pl.DeviceIdType.MESH
 N_Z = 4
 N_BLOCK = 2
+N_TAIL = 4
 
 
 def moe_kernel(x_hbm, ids_hbm, gates_hbm, wg_hbm, wu_hbm, wd_hbm, out_hbm,
@@ -130,7 +131,6 @@
     tok_far = remote(toks.at[1], toks.at[0], tok_send.at[0], tok_recv.at[0], ep=core_peer)
     tok_core.start()
     tok_y.start()
-    send_own(1)
 
     def zero(i, carry):
         rows = pl.ds(pl.multiple_of(i % N_BLOCK * block, block), block)
@@ -142,6 +142,7 @@
     for dist in range(1, N_Z):
         for t in range(3):
             event(0, dist, t)
+    send_own(1)
     for copy in own_copies:
         copy.wait()
     tok_y.wait_recv()
@@ -152,13 +153,7 @@
     wait_x(0)
     tok_far.wait_recv()
 
-    def place(i):
-        far = i < 2 * N_BLOCK
-        slot = jnp.where(far, i % 2, i // N_BLOCK)
-        row = jnp.where(far, i // 2, i % N_BLOCK)
-        return slot, row
-
-    def compute(e, slot, row):
+    def compute(e, slot, row, block):
         rows = pl.ds(pl.multiple_of(row * block, block), block)
         x = toks[slot, rows, :]
         a = jnp.dot(x, wg[e], preferred_element_type=jnp.float32)
@@ -176,27 +171,32 @@
     n_step = 4 * N_BLOCK * 2
 
     def packet(k, carry):
-        @pl.when(k + 2 < n_packet)
-        def _():
-            send_own(k + 2)
-
         def step(i, carry):
             for j in range(9):
                 @pl.when(i == j * n_step // 9)
                 def _():
                     event(k + 1, j // 3 + 1, j % 3)
-            slot, row = place(i // 2)
-            compute(2 * k + i % 2, slot, row)
+
+            @pl.when((i == 8 * n_step // 9) & (k + 2 < n_packet))
+            def _():
+                send_own(k + 2)
+            compute(2 * k + i % 2, i // 2 // N_BLOCK, i // 2 % N_BLOCK, block)
             return carry
 
         lax.fori_loop(0, n_step, step, 0)
-        wait_x(k + 1)
+
+        @pl.when(k + 2 < n_packet)
+        def _():
+            wait_x(k + 1)
         return carry
 
     lax.fori_loop(0, n_packet - 1, packet, 0)
 
+    tail = n_tok // N_TAIL
+    last = n_packet - 1
+
     def block_of(ref, row):
-        return ref.at[pl.ds(row * block, block), :]
+        return ref.at[pl.ds(row * tail, tail), :]
 
     def to_core(slot, row):
         return remote(block_of(acc.at[slot], row), block_of(from_core, row),
@@ -206,44 +206,58 @@
         return remote(block_of(acc.at[1], row), block_of(from_y, row),
                       sum_send.at[1, row], sum_recv.at[1, row], ep=y_peer)
 
-    def last_step(i, carry):
-        slot, row = place(i // 2)
-        compute(2 * (n_packet - 1) + i % 2, slot, row)
-        for n in range(N_BLOCK):
-            @pl.when(i == 4 * n + 1)
+    def far_first(i, carry):
+        compute(2 * last + r, i % 2, i // 2, block)
+        return carry
+
+    lax.fori_loop(0, 2 * N_BLOCK, far_first, 0)
+    wait_x(last)
+
+    def far_second(i, carry):
+        compute(2 * last + 1 - r, i % 2, i // 2, tail)
+        for n in range(N_TAIL):
+            @pl.when(i == 2 * n)
             def _():
                 to_core(0, n).start()
 
-            @pl.when(i == 4 * n + 3)
+            @pl.when(i == 2 * n + 1)
             def _():
                 to_core(0, n).wait_recv()
-                rows = slice(n * block, (n + 1) * block)
+                rows = slice(n * tail, (n + 1) * tail)
                 acc[1, rows, :] += from_core[rows, :]
                 to_y(n).start()
                 pl.semaphore_signal(credit.at[n], inc=1, device_id={'ep': core_peer}, device_id_type=MESH)
-
-            @pl.when(i == 4 * N_BLOCK + 2 * n + 1)
+        return carry
+
+    lax.fori_loop(0, 2 * N_TAIL, far_second, 0)
+
+    def near(i, carry):
+        compute(2 * last + i % 2, 2 + i // 2 // N_TAIL, i // 2 % N_TAIL, tail)
+        for n in range(N_TAIL):
+            @pl.when(i == 2 * n + 1)
             def _():
                 pl.semaphore_wait(credit.at[n], 1)
                 to_core(2, n).start()
         return carry
 
-    lax.fori_loop(0, n_step, last_step, 0)
+    lax.fori_loop(0, 4 * N_TAIL, near, 0)
 
     outs = []
-    for n in range(N_BLOCK):
-        rows = slice(n * block, (n + 1) * block)
+    for n in range(N_TAIL):
+        rows = slice(n * tail, (n + 1) * tail)
         to_core(2, n).wait_recv()
+        acc[3, rows, :] += toks[3, rows, :].astype(jnp.float32) + from_core[rows, :]
+    for n in range(N_TAIL):
+        rows = slice(n * tail, (n + 1) * tail)
         to_y(n).wait_recv()
-        y = toks[3, rows, :].astype(jnp.float32) + (acc[3, rows, :] + from_core[rows, :] + from_y[rows, :])
-        toks[3, rows, :] = y.astype(jnp.bfloat16)
+        toks[3, rows, :] = (acc[3, rows, :] + from_y[rows, :]).astype(jnp.bfloat16)
         copy = pltpu.make_async_copy(block_of(toks.at[3], n), block_of(out_hbm, n), out_sem.at[n])
         copy.start()
         outs.append(copy)
 
     for copy in meta + [tok_core, tok_y, tok_far]:
         copy.wait_send()
-    for n in range(N_BLOCK):
+    for n in range(N_TAIL):
         to_core(0, n).wait_send()
         to_y(n).wait_send()
         to_core(2, n).wait_send()
@@ -312,10 +326,10 @@
                 dma((3,)),
                 dma((2, 3)),
                 dma((2, 3)),
-                dma((3, N_BLOCK)),
-                dma((3, N_BLOCK)),
-                pltpu.SemaphoreType.REGULAR((N_BLOCK,)),
-                dma((N_BLOCK,)),
+                dma((3, N_TAIL)),
+                dma((3, N_TAIL)),
+                pltpu.SemaphoreType.REGULAR((N_TAIL,)),
+                dma((N_TAIL,)),
             ],
             compiler_params=pltpu.CompilerParams(
                 collective_id=0, has_side_effects=True, vmem_limit_bytes=67043328),

time: 340 us -> 320 us (0.941)
  Pallas kernels: 336 us -> 317 us
    pallas_call x1, Pallas kernels: 336 us -> 317 us  [device_step(): pl.pallas_call(moe_kernel, out_shape=jax.ShapeDtypeStruct((n_tok, d_model...]
where the time goes in v2:
time: 320 us
  Pallas kernels  317 us (99%)
    pallas_call x1, Pallas kernels, device_step(): pl.pallas_call(moe_kernel, out_shape=jax.ShapeDtypeStruct((n_tok, d_model...  317 us

profile of v2, /device:TPU:1, one launch (start us, length us, event | category | flops | bytes accessed | tf_op | source)
XLA Modules:
  0.0 320.1 jit_solution(9083768420504235762)
XLA Ops:
  0.0 317.0 %moe.1 = bf16[1024,1024]{1,0:T(8,128)(2,1)} custom-call(bf16[1024,1024]{1,0:T(8,128)(2,1)} %x_hbm.1, s32[8,1024]{1,0:T(8,128)} %bitcast.2, f32[8,1024]{1,0:T(8,128)} %bitcast.3, bf16[8,256,512]{2,1,0:T(8,128)(2,1)} %wg_hbm.1, bf16[8,256,512]{2,1,0:T(8,128)(2,1)} %wu_hbm.1, bf16[8,512,256]{2,1,0:T(8,128)(2,1)} %wd_hbm.1), custom_call_target="tpu_custom_call" | custom-call | flops 103079215104 | bytes 33554432 | tf_op jit(solution)/shard_map/moe/pallas_call | solution.py:304
  317.1 3.1 copy.8

commit v3 on v2

--- a/solution.py
+++ b/solution.py
@@ -16,7 +16,7 @@
 def moe_kernel(x_hbm, ids_hbm, gates_hbm, wg_hbm, wu_hbm, wd_hbm, out_hbm,
                wg, wu, wd, toks, ids, gates, acc, from_core, from_y,
                own_sem, recv_z, recv_x, send_r, send_l, send_x,
-               tok_send, tok_recv, meta_send, meta_recv,
+               tok_send, tok_recv, meta_send, meta_recv, home_send, home_recv, free,
                sum_send, sum_recv, credit, out_sem):
     r = lax.axis_index('rep')
     z = lax.axis_index('fsdp')
@@ -43,30 +43,48 @@
         return pltpu.make_async_remote_copy(src_ref=src, dst_ref=dst, send_sem=send_sem, recv_sem=recv_sem,
                                             device_id=where, device_id_type=MESH)
 
+    def place(k):
+        return 2 * (k % n_packet)
+
     def z_copy(t, k, s, right, own):
-        e = 2 * k + r
+        e = place(k) + r
         src = hbm[t].at[e] if own else shard(t, e, s)
         send = send_r if right else send_l
         to = (z + 1) % N_Z if right else (z + N_Z - 1) % N_Z
         return remote(src, shard(t, e, s), send.at[t, k, s], recv_z.at[t, k, s], fsdp=to)
 
     def x_copy(t, k, s):
-        e = 2 * k + r
+        e = place(k) + r
         return remote(shard(t, e, s), shard(t, e, s), send_x.at[t, k, s], recv_x.at[t, k, s], rep=1 - r)
 
     def x_arrival(t, k, s):
-        e = 2 * k + 1 - r
+        e = place(k) + 1 - r
         return remote(shard(t, e, s), shard(t, e, s), send_x.at[t, k, s], recv_x.at[t, k, s], rep=1 - r)
 
-    def send_own(k):
-        for t in range(3):
-            @pl.when(z > 0)
-            def _():
-                z_copy(t, k, z, False, True).start()
-
-            @pl.when(z < N_Z - 1)
-            def _():
-                z_copy(t, k, z, True, True).start()
+    def home_copy(t, q):
+        return remote(hbm[t].at[n_local - 2 + q], shard(t, q, z), home_send.at[t, q], home_recv.at[t, q], ep=y_peer)
+
+    def send_own(k, t, own=True):
+        @pl.when(z > 0)
+        def _():
+            z_copy(t, k, z, False, own).start()
+
+        @pl.when(z < N_Z - 1)
+        def _():
+            z_copy(t, k, z, True, own).start()
+
+    def signal_neighbours(sem, peers):
+        for peer in peers:
+            pl.semaphore_signal(sem, inc=1, device_id={'ep': peer}, device_id_type=MESH)
+        pl.semaphore_signal(sem, inc=1, device_id={'rep': 1 - r}, device_id_type=MESH)
+
+        @pl.when(z > 0)
+        def _():
+            pl.semaphore_signal(sem, inc=1, device_id={'fsdp': (z + N_Z - 1) % N_Z}, device_id_type=MESH)
+
+        @pl.when(z < N_Z - 1)
+        def _():
+            pl.semaphore_signal(sem, inc=1, device_id={'fsdp': (z + 1) % N_Z}, device_id_type=MESH)
 
     def event(k, dist, t):
         left = (z + N_Z - dist) % N_Z
@@ -96,17 +114,7 @@
                 x_arrival(t, k, (z + dist) % N_Z).wait_recv()
 
     barrier = pltpu.get_barrier_semaphore()
-    for peer in (core_peer, y_peer, far_peer):
-        pl.semaphore_signal(barrier, inc=1, device_id={'ep': peer}, device_id_type=MESH)
-    pl.semaphore_signal(barrier, inc=1, device_id={'rep': 1 - r}, device_id_type=MESH)
-
-    @pl.when(z > 0)
-    def _():
-        pl.semaphore_signal(barrier, inc=1, device_id={'fsdp': (z + N_Z - 1) % N_Z}, device_id_type=MESH)
-
-    @pl.when(z < N_Z - 1)
-    def _():
-        pl.semaphore_signal(barrier, inc=1, device_id={'fsdp': (z + 1) % N_Z}, device_id_type=MESH)
+    signal_neighbours(barrier, (core_peer, y_peer, far_peer))
 
     own_w = [pltpu.make_async_copy(hbm[t].at[e], shard(t, e, z), own_sem.at[t, e])
              for e in range(n_local) for t in range(3)]
@@ -117,7 +125,8 @@
     for copy in own_copies:
         copy.start()
 
-    pl.semaphore_wait(barrier, 4 + (z + N_Z - 1) // N_Z + (2 * N_Z - 2 - z) // N_Z)
+    z_peers = (z + N_Z - 1) // N_Z + (2 * N_Z - 2 - z) // N_Z
+    pl.semaphore_wait(barrier, 4 + z_peers)
 
     meta = []
     for slot, peer in ((2, core_peer), (1, y_peer), (0, far_peer)):
@@ -125,7 +134,8 @@
         meta.append(remote(gates_hbm, gates.at[slot], meta_send.at[1, slot], meta_recv.at[1, slot], ep=peer))
     for copy in meta:
         copy.start()
-    send_own(0)
+    for t in range(3):
+        send_own(0, t)
     tok_core = remote(x_hbm, toks.at[2], tok_send.at[2], tok_recv.at[2], ep=core_peer)
     tok_y = remote(x_hbm, toks.at[1], tok_send.at[1], tok_recv.at[1], ep=y_peer)
     tok_far = remote(toks.at[1], toks.at[0], tok_send.at[0], tok_recv.at[0], ep=core_peer)
@@ -142,7 +152,8 @@
     for dist in range(1, N_Z):
         for t in range(3):
             event(0, dist, t)
-    send_own(1)
+            if dist == 3:
+                send_own(1, t)
     for copy in own_copies:
         copy.wait()
     tok_y.wait_recv()
@@ -153,14 +164,14 @@
     wait_x(0)
     tok_far.wait_recv()
 
-    def compute(e, slot, row, block):
+    def compute(e, slot, row, block, group=None):
         rows = pl.ds(pl.multiple_of(row * block, block), block)
         x = toks[slot, rows, :]
         a = jnp.dot(x, wg[e], preferred_element_type=jnp.float32)
         b = jnp.dot(x, wu[e], preferred_element_type=jnp.float32)
         h = (a * jax.nn.sigmoid(a) * b).astype(jnp.bfloat16)
         o = jnp.dot(h, wd[e], preferred_element_type=jnp.float32).astype(jnp.bfloat16).astype(jnp.float32)
-        expert = p * n_local + e
+        expert = p * n_local + e if group is None else group * n_local + n_local - 2 + e
         chosen = jnp.where(ids[slot, :, rows] == expert, gates[slot, :, rows], 0.0)
         gate = jnp.sum(chosen, axis=0, keepdims=True)
         gate = jnp.broadcast_to(gate, (128, block)).T
@@ -168,32 +179,70 @@
             cols = slice(c * 128, (c + 1) * 128)
             acc[slot, rows, cols] += jnp.where(gate > 0, gate * o[:, cols], 0.0)
 
+    def drain(k, own=True):
+        for t in range(3):
+            @pl.when(z > 0)
+            def _():
+                z_copy(t, k, z, False, own).wait_send()
+
+            @pl.when(z < N_Z - 1)
+            def _():
+                z_copy(t, k, z, True, own).wait_send()
+            for dist in range(1, N_Z):
+                left = (z + N_Z - dist) % N_Z
+                right = (z + dist) % N_Z
+
+                @pl.when((z + dist < N_Z) & (z > 0))
+                def _():
+                    z_copy(t, k, right, False, False).wait_send()
+
+                @pl.when((z >= dist) & (z < N_Z - 1))
+                def _():
+                    z_copy(t, k, left, True, False).wait_send()
+                x_copy(t, k, (z + dist) % N_Z).wait_send()
+
+    def events(i, k, first, steps):
+        for n, at in enumerate(steps):
+            j = first + n
+
+            @pl.when(i == at)
+            def _():
+                event(k, j // 3 + 1, j % 3)
+
     n_step = 4 * N_BLOCK * 2
+    last = n_packet - 1
+    spread = [j * n_step // 9 for j in range(9)]
 
     def packet(k, carry):
         def step(i, carry):
             for j in range(9):
-                @pl.when(i == j * n_step // 9)
+                @pl.when(i == spread[j])
                 def _():
                     event(k + 1, j // 3 + 1, j % 3)
-
-            @pl.when((i == 8 * n_step // 9) & (k + 2 < n_packet))
-            def _():
-                send_own(k + 2)
+                    if j >= 6:
+                        send_own(k + 2, j - 6)
+
+            @pl.when((k == 1) & (i == 2))
+            def _():
+                pl.semaphore_wait(free, 2 + z_peers)
+                for q in range(2):
+                    for t in range(3):
+                        home_copy(t, q).start()
             compute(2 * k + i % 2, i // 2 // N_BLOCK, i // 2 % N_BLOCK, block)
             return carry
 
         lax.fori_loop(0, n_step, step, 0)
 
-        @pl.when(k + 2 < n_packet)
-        def _():
-            wait_x(k + 1)
-        return carry
-
-    lax.fori_loop(0, n_packet - 1, packet, 0)
+        @pl.when(k == 0)
+        def _():
+            wait_x(1)
+            drain(0)
+            signal_neighbours(free, (y_peer,))
+        return carry
+
+    lax.fori_loop(0, last - 1, packet, 0)
 
     tail = n_tok // N_TAIL
-    last = n_packet - 1
 
     def block_of(ref, row):
         return ref.at[pl.ds(row * tail, tail), :]
@@ -207,14 +256,16 @@
                       sum_send.at[1, row], sum_recv.at[1, row], ep=y_peer)
 
     def far_first(i, carry):
-        compute(2 * last + r, i % 2, i // 2, block)
+        events(i, last, 0, (0, 2))
+        compute(2 * last - 2 + r, i % 2, i // 2, block)
         return carry
 
     lax.fori_loop(0, 2 * N_BLOCK, far_first, 0)
-    wait_x(last)
+    wait_x(last - 1)
 
     def far_second(i, carry):
-        compute(2 * last + 1 - r, i % 2, i // 2, tail)
+        events(i, last, 2, (1, 4, 7))
+        compute(2 * last - 1 - r, i % 2, i // 2, tail)
         for n in range(N_TAIL):
             @pl.when(i == 2 * n)
             def _():
@@ -232,15 +283,43 @@
     lax.fori_loop(0, 2 * N_TAIL, far_second, 0)
 
     def near(i, carry):
-        compute(2 * last + i % 2, 2 + i // 2 // N_TAIL, i // 2 % N_TAIL, tail)
+        events(i, last, 5, (1, 2, 4, 6))
+        for t, at in enumerate((2, 4, 6)):
+            @pl.when(i == at)
+            def _():
+                for q in range(2):
+                    home_copy(t, q).wait_recv()
+                send_own(n_packet, t, False)
+        compute(2 * last - 2 + i % 2, 2 + i // 2 // N_BLOCK, i // 2 % N_BLOCK, block)
+        return carry
+
+    lax.fori_loop(0, 4 * N_BLOCK, near, 0)
+    wait_x(last)
+
+    def home(i, carry):
+        events(i, n_packet, 0, [j * 4 * N_BLOCK // 9 for j in range(9)])
+        compute(2 * last + i % 2, 2 + i // 2 // N_BLOCK, i // 2 % N_BLOCK, block)
+        return carry
+
+    lax.fori_loop(0, 4 * N_BLOCK, home, 0)
+
+    def peer_first(i, carry):
+        compute(r, 2 + i // N_BLOCK, i % N_BLOCK, block, y_peer)
+        return carry
+
+    lax.fori_loop(0, 2 * N_BLOCK, peer_first, 0)
+    wait_x(n_packet)
+
+    def peer_second(i, carry):
+        compute(1 - r, 2 + i // N_TAIL, i % N_TAIL, tail, y_peer)
         for n in range(N_TAIL):
-            @pl.when(i == 2 * n + 1)
+            @pl.when(i == n)
             def _():
                 pl.semaphore_wait(credit.at[n], 1)
                 to_core(2, n).start()
         return carry
 
-    lax.fori_loop(0, 4 * N_TAIL, near, 0)
+    lax.fori_loop(0, 2 * N_TAIL, peer_second, 0)
 
     outs = []
     for n in range(N_TAIL):
@@ -262,30 +341,16 @@
         to_y(n).wait_send()
         to_core(2, n).wait_send()
 
-    def drain(k, carry):
-        for t in range(3):
-            @pl.when(z > 0)
-            def _():
-                z_copy(t, k, z, False, True).wait_send()
-
-            @pl.when(z < N_Z - 1)
-            def _():
-                z_copy(t, k, z, True, True).wait_send()
-            for dist in range(1, N_Z):
-                left = (z + N_Z - dist) % N_Z
-                right = (z + dist) % N_Z
-
-                @pl.when((z + dist < N_Z) & (z > 0))
-                def _():
-                    z_copy(t, k, right, False, False).wait_send()
-
-                @pl.when((z >= dist) & (z < N_Z - 1))
-                def _():
-                    z_copy(t, k, left, True, False).wait_send()
-                x_copy(t, k, (z + dist) % N_Z).wait_send()
-        return carry
-
-    lax.fori_loop(0, n_packet, drain, 0)
+    for t in range(3):
+        for q in range(2):
+            home_copy(t, q).wait_send()
+
+    def drain_step(k, carry):
+        drain(k)
+        return carry
+
+    lax.fori_loop(1, n_packet, drain_step, 0)
+    drain(n_packet, False)
     for copy in outs:
         copy.wait()
 
@@ -317,15 +382,18 @@
                 pltpu.VMEM((n_tok, d_model), jnp.float32),
                 pltpu.VMEM((n_tok, d_model), jnp.float32),
                 dma((4, n_local)),
-                dma((3, n_packet, N_Z)),
-                dma((3, n_packet, N_Z)),
-                dma((3, n_packet, N_Z)),
-                dma((3, n_packet, N_Z)),
-                dma((3, n_packet, N_Z)),
+                dma((3, n_packet + 1, N_Z)),
+                dma((3, n_packet + 1, N_Z)),
+                dma((3, n_packet + 1, N_Z)),
+                dma((3, n_packet + 1, N_Z)),
+                dma((3, n_packet + 1, N_Z)),
                 dma((3,)),
                 dma((3,)),
                 dma((2, 3)),
                 dma((2, 3)),
+                dma((3, 2)),
+                dma((3, 2)),
+                pltpu.SemaphoreType.REGULAR,
                 dma((3, N_TAIL)),
                 dma((3, N_TAIL)),
                 pltpu.SemaphoreType.REGULAR((N_TAIL,)),

time: 320 us -> 285 us (0.89)
  Pallas kernels: 317 us -> 281 us
    pallas_call x1, Pallas kernels: 317 us -> 281 us  [device_step(): pl.pallas_call(moe_kernel, out_shape=jax.ShapeDtypeStruct((n_tok, d_model...]
where the time goes in v3:
time: 285 us; the launch traced here: 284 us
  Pallas kernels  281 us (99%)
  local copies, waits for them, and re-layouts  3.08 us (1%)
    pallas_call x1, Pallas kernels, device_step(): pl.pallas_call(moe_kernel, out_shape=jax.ShapeDtypeStruct((n_tok, d_model...  281 us

profile of v3, /device:TPU:1, one launch (start us, length us, event | category | flops | bytes accessed | tf_op | source)
XLA Modules:
  0.0 284.0 jit_solution(3192484207437733352)
XLA Ops:
  0.0 281.0 %moe.1 = bf16[1024,1024]{1,0:T(8,128)(2,1)} custom-call(bf16[1024,1024]{1,0:T(8,128)(2,1)} %x_hbm.1, s32[8,1024]{1,0:T(8,128)} %bitcast.2, f32[8,1024]{1,0:T(8,128)} %bitcast.3, bf16[8,256,512]{2,1,0:T(8,128)(2,1)} %wg_hbm.1, bf16[8,256,512]{2,1,0:T(8,128)(2,1)} %wu_hbm.1, bf16[8,512,256]{2,1,0:T(8,128)(2,1)} %wd_hbm.1), custom_call_target="tpu_custom_call" | custom-call | flops 103079215104 | bytes 33554432 | tf_op jit(solution)/shard_map/moe/pallas_call | solution.py:369
  281.0 3.1 %copy.8 = bf16[1024,1024]{1,0:T(8,128)(2,1)} copy(bf16[1024,1024]{1,0:T(8,128)(2,1)} %moe.1) | data formatting | bytes 4194304

commit v4 on v3

--- a/solution.py
+++ b/solution.py
@@ -11,6 +11,13 @@
 N_Z = 4
 N_BLOCK = 2
 N_TAIL = 4
+N_EVENT = 9
+LEAD = 2
+STEP_OF = (0, 0, 3, 4, 6, 9, 12, 13, 15)
+STEP_OF_LAST = (2, 5, 6, 6, 8, 11, 12, 15, 17)
+STEP_OF_PEER = (0, 0, 1, 3, 5, 8, 10, 13, 14)
+OWN_AFTER = (5, 6, 7)
+PEER_OWN_AFTER = (6, 10, 13)
 
 
 def moe_kernel(x_hbm, ids_hbm, gates_hbm, wg_hbm, wu_hbm, wd_hbm, out_hbm,
@@ -86,7 +93,9 @@
         def _():
             pl.semaphore_signal(sem, inc=1, device_id={'fsdp': (z + 1) % N_Z}, device_id_type=MESH)
 
-    def event(k, dist, t):
+    def event(k, j):
+        peer_packet = isinstance(k, int) and k == n_packet
+        dist, t = (j % 3 + 1, j // 3) if peer_packet else (j // 3 + 1, j % 3)
         left = (z + N_Z - dist) % N_Z
         right = (z + dist) % N_Z
 
@@ -108,9 +117,18 @@
                 z_copy(t, k, left, True, False).start()
             x_copy(t, k, left).start()
 
-    def wait_x(k):
+        last_packets = isinstance(k, int) and k >= n_packet - 1
+        for t in range(3):
+            if not last_packets and OWN_AFTER[t] == j:
+                send_own(k + 1, t)
+            if last_packets and PEER_OWN_AFTER[t] == (k - n_packet + 1) * N_EVENT + j:
+                for q in range(2):
+                    home_copy(t, q).wait_recv()
+                send_own(n_packet, t, False)
+
+    def wait_x(k, tensors=(0, 1, 2)):
         for dist in range(1, N_Z):
-            for t in range(3):
+            for t in tensors:
                 x_arrival(t, k, (z + dist) % N_Z).wait_recv()
 
     barrier = pltpu.get_barrier_semaphore()
@@ -149,11 +167,8 @@
 
     lax.fori_loop(0, 4 * N_BLOCK, zero, 0)
 
-    for dist in range(1, N_Z):
-        for t in range(3):
-            event(0, dist, t)
-            if dist == 3:
-                send_own(1, t)
+    for j in range(N_EVENT):
+        event(0, j)
     for copy in own_copies:
         copy.wait()
     tok_y.wait_recv()
@@ -161,23 +176,45 @@
     for copy in meta:
         copy.wait_recv()
     tok_core.wait_recv()
+    for j in range(LEAD):
+        event(1, j)
     wait_x(0)
     tok_far.wait_recv()
 
-    def compute(e, slot, row, block, group=None):
-        rows = pl.ds(pl.multiple_of(row * block, block), block)
+    def hidden(e, slot, rows):
         x = toks[slot, rows, :]
         a = jnp.dot(x, wg[e], preferred_element_type=jnp.float32)
         b = jnp.dot(x, wu[e], preferred_element_type=jnp.float32)
-        h = (a * jax.nn.sigmoid(a) * b).astype(jnp.bfloat16)
-        o = jnp.dot(h, wd[e], preferred_element_type=jnp.float32).astype(jnp.bfloat16).astype(jnp.float32)
-        expert = p * n_local + e if group is None else group * n_local + n_local - 2 + e
+        return (a * jax.nn.sigmoid(a) * b).astype(jnp.bfloat16)
+
+    def add_output(h, w_down, expert, slot, rows, start, width):
+        o = jnp.dot(h, w_down, preferred_element_type=jnp.float32).astype(jnp.bfloat16).astype(jnp.float32)
         chosen = jnp.where(ids[slot, :, rows] == expert, gates[slot, :, rows], 0.0)
         gate = jnp.sum(chosen, axis=0, keepdims=True)
-        gate = jnp.broadcast_to(gate, (128, block)).T
-        for c in range(acc.shape[2] // 128):
-            cols = slice(c * 128, (c + 1) * 128)
-            acc[slot, rows, cols] += jnp.where(gate > 0, gate * o[:, cols], 0.0)
+        gate = jnp.broadcast_to(gate, (128, h.shape[0])).T
+        for c in range(width // 128):
+            cols = pl.ds(start + c * 128, 128)
+            acc[slot, rows, cols] += jnp.where(gate > 0, gate * o[:, c * 128:(c + 1) * 128], 0.0)
+
+    def rows_of(row, block):
+        return pl.ds(pl.multiple_of(row * block, block), block)
+
+    def compute(e, slot, row, block):
+        rows = rows_of(row, block)
+        add_output(hidden(e, slot, rows), wd[e], p * n_local + e, slot, rows, 0, acc.shape[2])
+
+    ffn = wg.shape[2]
+
+    def peer_hidden(e, slot, row):
+        rows = rows_of(row, block)
+        toks[slot - 2, rows, pl.ds(pl.multiple_of(e * ffn, ffn), ffn)] = hidden(e, slot, rows)
+
+    def peer_output(e, slot, row, s):
+        rows = rows_of(row, block)
+        start = pl.multiple_of(s * d_shard, d_shard)
+        h = toks[slot - 2, rows, pl.ds(pl.multiple_of(e * ffn, ffn), ffn)]
+        expert = y_peer * n_local + n_local - 2 + e
+        add_output(h, wd[e, :, pl.ds(start, d_shard)], expert, slot, rows, start, d_shard)
 
     def drain(k, own=True):
         for t in range(3):
@@ -201,32 +238,25 @@
                     z_copy(t, k, left, True, False).wait_send()
                 x_copy(t, k, (z + dist) % N_Z).wait_send()
 
-    def events(i, k, first, steps):
-        for n, at in enumerate(steps):
-            j = first + n
-
-            @pl.when(i == at)
-            def _():
-                event(k, j // 3 + 1, j % 3)
+    def events(i, k, steps, first=0, offset=0):
+        for j in range(first, N_EVENT):
+            if steps[j] >= offset:
+                @pl.when(i == steps[j] - offset)
+                def _():
+                    event(k, j)
 
     n_step = 4 * N_BLOCK * 2
     last = n_packet - 1
-    spread = [j * n_step // 9 for j in range(9)]
 
     def packet(k, carry):
         def step(i, carry):
-            for j in range(9):
-                @pl.when(i == spread[j])
-                def _():
-                    event(k + 1, j // 3 + 1, j % 3)
-                    if j >= 6:
-                        send_own(k + 2, j - 6)
+            events(i, k + 1, STEP_OF, LEAD)
 
             @pl.when((k == 1) & (i == 2))
             def _():
                 pl.semaphore_wait(free, 2 + z_peers)
-                for q in range(2):
-                    for t in range(3):
+                for t in range(3):
+                    for q in range(2):
                         home_copy(t, q).start()
             compute(2 * k + i % 2, i // 2 // N_BLOCK, i // 2 % N_BLOCK, block)
             return carry
@@ -235,6 +265,8 @@
 
         @pl.when(k == 0)
         def _():
+            for j in range(LEAD):
+                event(2, j)
             wait_x(1)
             drain(0)
             signal_neighbours(free, (y_peer,))
@@ -247,16 +279,26 @@
     def block_of(ref, row):
         return ref.at[pl.ds(row * tail, tail), :]
 
-    def to_core(slot, row):
-        return remote(block_of(acc.at[slot], row), block_of(from_core, row),
-                      sum_send.at[slot, row], sum_recv.at[slot, row], ep=core_peer)
+    def to_core(row):
+        return remote(block_of(acc.at[0], row), block_of(from_core, row),
+                      sum_send.at[0, row], sum_recv.at[0, row], ep=core_peer)
+
+    def shard_at(n):
+        return (z + n + z // 2 * (N_Z - 2 * n)) % N_Z
+
+    def columns(n):
+        return pl.ds(pl.multiple_of(shard_at(n) * d_shard, d_shard), d_shard)
+
+    def to_core_near(n):
+        return remote(acc.at[2, :, columns(n)], from_core.at[:, columns(n)],
+                      sum_send.at[2, n], sum_recv.at[2, n], ep=core_peer)
 
     def to_y(row):
         return remote(block_of(acc.at[1], row), block_of(from_y, row),
                       sum_send.at[1, row], sum_recv.at[1, row], ep=y_peer)
 
     def far_first(i, carry):
-        events(i, last, 0, (0, 2))
+        events(i, last, STEP_OF_LAST)
         compute(2 * last - 2 + r, i % 2, i // 2, block)
         return carry
 
@@ -264,16 +306,16 @@
     wait_x(last - 1)
 
     def far_second(i, carry):
-        events(i, last, 2, (1, 4, 7))
+        events(i, last, STEP_OF_LAST, offset=2 * N_BLOCK)
         compute(2 * last - 1 - r, i % 2, i // 2, tail)
         for n in range(N_TAIL):
             @pl.when(i == 2 * n)
             def _():
-                to_core(0, n).start()
+                to_core(n).start()
 
             @pl.when(i == 2 * n + 1)
             def _():
-                to_core(0, n).wait_recv()
+                to_core(n).wait_recv()
                 rows = slice(n * tail, (n + 1) * tail)
                 acc[1, rows, :] += from_core[rows, :]
                 to_y(n).start()
@@ -283,63 +325,71 @@
     lax.fori_loop(0, 2 * N_TAIL, far_second, 0)
 
     def near(i, carry):
-        events(i, last, 5, (1, 2, 4, 6))
-        for t, at in enumerate((2, 4, 6)):
-            @pl.when(i == at)
-            def _():
-                for q in range(2):
-                    home_copy(t, q).wait_recv()
-                send_own(n_packet, t, False)
+        events(i, last, STEP_OF_LAST, offset=2 * N_BLOCK + 2 * N_TAIL)
         compute(2 * last - 2 + i % 2, 2 + i // 2 // N_BLOCK, i // 2 % N_BLOCK, block)
         return carry
 
     lax.fori_loop(0, 4 * N_BLOCK, near, 0)
+    for j in range(LEAD):
+        event(n_packet, j)
     wait_x(last)
 
     def home(i, carry):
-        events(i, n_packet, 0, [j * 4 * N_BLOCK // 9 for j in range(9)])
+        events(i, n_packet, STEP_OF_PEER, LEAD)
         compute(2 * last + i % 2, 2 + i // 2 // N_BLOCK, i // 2 % N_BLOCK, block)
         return carry
 
     lax.fori_loop(0, 4 * N_BLOCK, home, 0)
+    tok_far.wait_send()
 
     def peer_first(i, carry):
-        compute(r, 2 + i // N_BLOCK, i % N_BLOCK, block, y_peer)
+        events(i, n_packet, STEP_OF_PEER, LEAD, offset=4 * N_BLOCK)
+        peer_hidden(r, 2 + i // N_BLOCK, i % N_BLOCK)
         return carry
 
     lax.fori_loop(0, 2 * N_BLOCK, peer_first, 0)
-    wait_x(n_packet)
+    wait_x(n_packet, (0, 1))
 
     def peer_second(i, carry):
-        compute(1 - r, 2 + i // N_TAIL, i % N_TAIL, tail, y_peer)
-        for n in range(N_TAIL):
-            @pl.when(i == n)
-            def _():
-                pl.semaphore_wait(credit.at[n], 1)
-                to_core(2, n).start()
-        return carry
-
-    lax.fori_loop(0, 2 * N_TAIL, peer_second, 0)
-
+        events(i, n_packet, STEP_OF_PEER, LEAD, offset=6 * N_BLOCK)
+        peer_hidden(1 - r, 2 + i // N_BLOCK, i % N_BLOCK)
+        return carry
+
+    lax.fori_loop(0, 2 * N_BLOCK, peer_second, 0)
+    for n in range(N_TAIL):
+        pl.semaphore_wait(credit.at[n], 1)
+
+    for n in range(N_Z):
+        s = shard_at(n)
+        if n > 0:
+            x_arrival(2, n_packet, s).wait_recv()
+        for slot in (2, 3):
+            def output(i, carry):
+                peer_output(i % 2, slot, i // 2, s)
+                return carry
+
+            lax.fori_loop(0, 2 * N_BLOCK, output, 0)
+            if slot == 2:
+                to_core_near(n).start()
+
+    for n in range(N_TAIL):
+        to_y(n).wait_recv()
     outs = []
-    for n in range(N_TAIL):
-        rows = slice(n * tail, (n + 1) * tail)
-        to_core(2, n).wait_recv()
-        acc[3, rows, :] += toks[3, rows, :].astype(jnp.float32) + from_core[rows, :]
-    for n in range(N_TAIL):
-        rows = slice(n * tail, (n + 1) * tail)
-        to_y(n).wait_recv()
-        toks[3, rows, :] = (acc[3, rows, :] + from_y[rows, :]).astype(jnp.bfloat16)
-        copy = pltpu.make_async_copy(block_of(toks.at[3], n), block_of(out_hbm, n), out_sem.at[n])
+    for n in range(N_Z):
+        to_core_near(n).wait_recv()
+        cols = columns(n)
+        y = toks[3, :, cols].astype(jnp.float32) + (acc[3, :, cols] + from_core[:, cols] + from_y[:, cols])
+        toks[3, :, cols] = y.astype(jnp.bfloat16)
+        copy = pltpu.make_async_copy(toks.at[3, :, cols], out_hbm.at[:, cols], out_sem.at[n])
         copy.start()
         outs.append(copy)
 
-    for copy in meta + [tok_core, tok_y, tok_far]:
+    for copy in meta + [tok_core, tok_y]:
         copy.wait_send()
     for n in range(N_TAIL):
-        to_core(0, n).wait_send()
+        to_core(n).wait_send()
         to_y(n).wait_send()
-        to_core(2, n).wait_send()
+        to_core_near(n).wait_send()
 
     for t in range(3):
         for q in range(2):

time: 285 us -> 282 us (0.989)
  no operation moved by 1% of the time
where the time goes in v4:
time: 282 us
  Pallas kernels  279 us (99%)
  local copies, waits for them, and re-layouts  3.08 us (1%)
    pallas_call x1, Pallas kernels, device_step(): pl.pallas_call(moe_kernel, out_shape=jax.ShapeDtypeStruct((n_tok, d_model...  279 us

profile of v4, /device:TPU:1, one launch (start us, length us, event | category | flops | bytes accessed | tf_op | source)
XLA Modules:
  0.0 281.6 jit_solution(2511284073130857951)
XLA Ops:
  0.0 278.5 %moe.1 = bf16[1024,1024]{1,0:T(8,128)(2,1)} custom-call(bf16[1024,1024]{1,0:T(8,128)(2,1)} %x_hbm.1, s32[8,1024]{1,0:T(8,128)} %bitcast.2, f32[8,1024]{1,0:T(8,128)} %bitcast.3, bf16[8,256,512]{2,1,0:T(8,128)(2,1)} %wg_hbm.1, bf16[8,256,512]{2,1,0:T(8,128)(2,1)} %wu_hbm.1, bf16[8,512,256]{2,1,0:T(8,128)(2,1)} %wd_hbm.1), custom_call_target="tpu_custom_call" | custom-call | flops 103079215104 | bytes 33554432 | tf_op jit(solution)/shard_map/moe/pallas_call | solution.py:419
  278.5 3.1 %copy.8 = bf16[1024,1024]{1,0:T(8,128)(2,1)} copy(bf16[1024,1024]{1,0:T(8,128)(2,1)} %moe.1) | data formatting | bytes 4194304

commit v5 on v4

--- a/solution.py
+++ b/solution.py
@@ -15,7 +15,7 @@
 LEAD = 2
 STEP_OF = (0, 0, 3, 4, 6, 9, 12, 13, 15)
 STEP_OF_LAST = (2, 5, 6, 6, 8, 11, 12, 15, 17)
-STEP_OF_PEER = (0, 0, 1, 3, 5, 8, 10, 13, 14)
+STEP_OF_PEER = (0, 0, 1, 3, 5, 8, 10, 14, 16)
 OWN_AFTER = (5, 6, 7)
 PEER_OWN_AFTER = (6, 10, 13)
 
@@ -209,15 +209,20 @@
         rows = rows_of(row, block)
         toks[slot - 2, rows, pl.ds(pl.multiple_of(e * ffn, ffn), ffn)] = hidden(e, slot, rows)
 
-    def peer_output(e, slot, row, s):
-        rows = rows_of(row, block)
-        start = pl.multiple_of(s * d_shard, d_shard)
-        h = toks[slot - 2, rows, pl.ds(pl.multiple_of(e * ffn, ffn), ffn)]
+    def peer_output(e, slot, n):
+        start = pl.multiple_of(shard_at(n) * d_shard, d_shard)
+        h = toks[slot - 2, :, pl.ds(pl.multiple_of(e * ffn, ffn), ffn)]
         expert = y_peer * n_local + n_local - 2 + e
-        add_output(h, wd[e, :, pl.ds(start, d_shard)], expert, slot, rows, start, d_shard)
-
-    def drain(k, own=True):
-        for t in range(3):
+        add_output(h, wd[e, :, pl.ds(start, d_shard)], expert, slot, pl.ds(0, n_tok), start, d_shard)
+
+    def shard_at(n):
+        return (z + n + z // 2 * (N_Z - 2 * n)) % N_Z
+
+    def columns(n):
+        return pl.ds(pl.multiple_of(shard_at(n) * d_shard, d_shard), d_shard)
+
+    def drain(k, own=True, tensors=(0, 1, 2)):
+        for t in tensors:
             @pl.when(z > 0)
             def _():
                 z_copy(t, k, z, False, own).wait_send()
@@ -283,12 +288,6 @@
         return remote(block_of(acc.at[0], row), block_of(from_core, row),
                       sum_send.at[0, row], sum_recv.at[0, row], ep=core_peer)
 
-    def shard_at(n):
-        return (z + n + z // 2 * (N_Z - 2 * n)) % N_Z
-
-    def columns(n):
-        return pl.ds(pl.multiple_of(shard_at(n) * d_shard, d_shard), d_shard)
-
     def to_core_near(n):
         return remote(acc.at[2, :, columns(n)], from_core.at[:, columns(n)],
                       sum_send.at[2, n], sum_recv.at[2, n], ep=core_peer)
@@ -330,6 +329,12 @@
         return carry
 
     lax.fori_loop(0, 4 * N_BLOCK, near, 0)
+
+    def drain_step(k, carry):
+        drain(k)
+        return carry
+
+    lax.fori_loop(1, last, drain_step, 0)
     for j in range(LEAD):
         event(n_packet, j)
     wait_x(last)
@@ -340,7 +345,8 @@
         return carry
 
     lax.fori_loop(0, 4 * N_BLOCK, home, 0)
-    tok_far.wait_send()
+    for copy in meta + [tok_core, tok_y, tok_far]:
+        copy.wait_send()
 
     def peer_first(i, carry):
         events(i, n_packet, STEP_OF_PEER, LEAD, offset=4 * N_BLOCK)
@@ -359,48 +365,52 @@
     for n in range(N_TAIL):
         pl.semaphore_wait(credit.at[n], 1)
 
-    for n in range(N_Z):
-        s = shard_at(n)
-        if n > 0:
-            x_arrival(2, n_packet, s).wait_recv()
-        for slot in (2, 3):
-            def output(i, carry):
-                peer_output(i % 2, slot, i // 2, s)
-                return carry
-
-            lax.fori_loop(0, 2 * N_BLOCK, output, 0)
-            if slot == 2:
-                to_core_near(n).start()
-
-    for n in range(N_TAIL):
-        to_y(n).wait_recv()
-    outs = []
-    for n in range(N_Z):
+    def outputs(e, n, complete):
+        def output(i, carry):
+            peer_output(e, 2 + i, n)
+            if complete:
+                @pl.when(i == 0)
+                def _():
+                    to_core_near(n).start()
+            return carry
+
+        lax.fori_loop(0, 2, output, 0)
+
+    def finish(n):
         to_core_near(n).wait_recv()
         cols = columns(n)
         y = toks[3, :, cols].astype(jnp.float32) + (acc[3, :, cols] + from_core[:, cols] + from_y[:, cols])
         toks[3, :, cols] = y.astype(jnp.bfloat16)
         copy = pltpu.make_async_copy(toks.at[3, :, cols], out_hbm.at[:, cols], out_sem.at[n])
         copy.start()
-        outs.append(copy)
-
-    for copy in meta + [tok_core, tok_y]:
-        copy.wait_send()
-    for n in range(N_TAIL):
-        to_core(n).wait_send()
-        to_y(n).wait_send()
-        to_core_near(n).wait_send()
-
+        return copy
+
+    outputs(r, 0, False)
+    outputs(1 - r, 0, True)
+    outputs(r, 1, False)
+    event(n_packet, N_EVENT - 1)
+    x_arrival(2, n_packet, shard_at(1)).wait_recv()
+    outputs(1 - r, 1, True)
+    outputs(r, 2, False)
+    outputs(r, 3, False)
+    x_arrival(2, n_packet, shard_at(2)).wait_recv()
+    outputs(1 - r, 2, True)
+    drain(last)
+    drain(n_packet, False, (0, 1))
     for t in range(3):
         for q in range(2):
             home_copy(t, q).wait_send()
-
-    def drain_step(k, carry):
-        drain(k)
-        return carry
-
-    lax.fori_loop(1, n_packet, drain_step, 0)
-    drain(n_packet, False)
+    for n in range(N_TAIL):
+        to_y(n).wait_recv()
+        to_core(n).wait_send()
+        to_y(n).wait_send()
+    outs = [finish(n) for n in range(2)]
+    x_arrival(2, n_packet, shard_at(3)).wait_recv()
+    outputs(1 - r, 3, True)
+    outs += [finish(n) for n in range(2, N_Z)]
+    drain(n_packet, False, (2,))
+    for n in range(N_Z):
+        to_core_near(n).wait_send()
     for copy in outs:
         copy.wait()
 

time: 282 us -> 278 us (0.986)
  Pallas kernels: 279 us -> 274 us
    pallas_call x1, Pallas kernels: 279 us -> 274 us  [device_step(): pl.pallas_call(moe_kernel, out_shape=jax.ShapeDtypeStruct((n_tok, d_model...]
where the time goes in v5:
time: 278 us; the launch traced here: 277 us
  Pallas kernels  274 us (99%)
  local copies, waits for them, and re-layouts  3.08 us (1%)
    pallas_call x1, Pallas kernels, device_step(): pl.pallas_call(moe_kernel, out_shape=jax.ShapeDtypeStruct((n_tok, d_model...  274 us

profile of v5, /device:TPU:1, one launch (start us, length us, event | category | flops | bytes accessed | tf_op | source)
XLA Modules:
  0.0 277.1 jit_solution(180846663535901810)
XLA Ops:
  0.0 274.0 %moe.1 = bf16[1024,1024]{1,0:T(8,128)(2,1)} custom-call(bf16[1024,1024]{1,0:T(8,128)(2,1)} %x_hbm.1, s32[8,1024]{1,0:T(8,128)} %bitcast.2, f32[8,1024]{1,0:T(8,128)} %bitcast.3, bf16[8,256,512]{2,1,0:T(8,128)(2,1)} %wg_hbm.1, bf16[8,256,512]{2,1,0:T(8,128)(2,1)} %wu_hbm.1, bf16[8,512,256]{2,1,0:T(8,128)(2,1)} %wd_hbm.1), custom_call_target="tpu_custom_call" | custom-call | flops 103079215104 | bytes 33554432 | tf_op jit(solution)/shard_map/moe/pallas_call | solution.py:429
  274.0 3.1 %copy.8 = bf16[1024,1024]{1,0:T(8,128)(2,1)} copy(bf16[1024,1024]{1,0:T(8,128)(2,1)} %moe.1) | data formatting | bytes 4194304

commit v6 on v5

--- a/solution.py
+++ b/solution.py
@@ -13,6 +13,7 @@
 N_TAIL = 4
 N_EVENT = 9
 LEAD = 2
+N_PART = 4
 STEP_OF = (0, 0, 3, 4, 6, 9, 12, 13, 15)
 STEP_OF_LAST = (2, 5, 6, 6, 8, 11, 12, 15, 17)
 STEP_OF_PEER = (0, 0, 1, 3, 5, 8, 10, 14, 16)
@@ -20,11 +21,11 @@
 PEER_OWN_AFTER = (6, 10, 13)
 
 
-def moe_kernel(x_hbm, ids_hbm, gates_hbm, wg_hbm, wu_hbm, wd_hbm, out_hbm,
+def moe_kernel(x_hbm, ids_hbm, gates_hbm, wg_hbm, wu_hbm, wd_hbm, out_ref,
                wg, wu, wd, toks, ids, gates, acc, from_core, from_y,
                own_sem, recv_z, recv_x, send_r, send_l, send_x,
                tok_send, tok_recv, meta_send, meta_recv, home_send, home_recv, free,
-               sum_send, sum_recv, credit, out_sem):
+               sum_send, sum_recv, credit):
     r = lax.axis_index('rep')
     z = lax.axis_index('fsdp')
     p = lax.axis_index('ep')
@@ -40,12 +41,21 @@
 
     hbm = (wg_hbm, wu_hbm, wd_hbm)
 
-    def shard(t, e, s):
+    def shard(t, e, s, k=0):
         start = pl.multiple_of(s * d_shard, d_shard)
+        if is_peer(k) and t >= 2:
+            part = wd.shape[1] // N_PART
+            return wd.at[e, pl.ds((t - 2) * part, part), pl.ds(start, d_shard)]
         if t == 2:
             return wd.at[e, :, pl.ds(start, d_shard)]
         return (wg, wu)[t].at[e, pl.ds(start, d_shard), :]
 
+    def is_peer(k):
+        return isinstance(k, int) and k == n_packet
+
+    def parts(k, t):
+        return range(2, 2 + N_PART) if is_peer(k) and t == 2 else (t,)
+
     def remote(src, dst, send_sem, recv_sem, **where):
         return pltpu.make_async_remote_copy(src_ref=src, dst_ref=dst, send_sem=send_sem, recv_sem=recv_sem,
                                             device_id=where, device_id_type=MESH)
@@ -54,19 +64,19 @@
         return 2 * (k % n_packet)
 
     def z_copy(t, k, s, right, own):
-        e = place(k) + r
-        src = hbm[t].at[e] if own else shard(t, e, s)
+        here = shard(t, place(k) + r, s, k)
+        src = hbm[t].at[place(k) + r] if own else here
         send = send_r if right else send_l
         to = (z + 1) % N_Z if right else (z + N_Z - 1) % N_Z
-        return remote(src, shard(t, e, s), send.at[t, k, s], recv_z.at[t, k, s], fsdp=to)
+        return remote(src, here, send.at[t, k, s], recv_z.at[t, k, s], fsdp=to)
 
     def x_copy(t, k, s):
-        e = place(k) + r
-        return remote(shard(t, e, s), shard(t, e, s), send_x.at[t, k, s], recv_x.at[t, k, s], rep=1 - r)
+        here = shard(t, place(k) + r, s, k)
+        return remote(here, here, send_x.at[t, k, s], recv_x.at[t, k, s], rep=1 - r)
 
     def x_arrival(t, k, s):
-        e = place(k) + 1 - r
-        return remote(shard(t, e, s), shard(t, e, s), send_x.at[t, k, s], recv_x.at[t, k, s], rep=1 - r)
+        here = shard(t, place(k) + 1 - r, s, k)
+        return remote(here, here, send_x.at[t, k, s], recv_x.at[t, k, s], rep=1 - r)
 
     def home_copy(t, q):
         return remote(hbm[t].at[n_local - 2 + q], shard(t, q, z), home_send.at[t, q], home_recv.at[t, q], ep=y_peer)
@@ -74,11 +84,13 @@
     def send_own(k, t, own=True):
         @pl.when(z > 0)
         def _():
-            z_copy(t, k, z, False, own).start()
+            for u in parts(k, t):
+                z_copy(u, k, z, False, own).start()
 
         @pl.when(z < N_Z - 1)
         def _():
-            z_copy(t, k, z, True, own).start()
+            for u in parts(k, t):
+                z_copy(u, k, z, True, own).start()
 
     def signal_neighbours(sem, peers):
         for peer in peers:
@@ -94,28 +106,27 @@
             pl.semaphore_signal(sem, inc=1, device_id={'fsdp': (z + 1) % N_Z}, device_id_type=MESH)
 
     def event(k, j):
-        peer_packet = isinstance(k, int) and k == n_packet
-        dist, t = (j % 3 + 1, j // 3) if peer_packet else (j // 3 + 1, j % 3)
+        dist, t = (j % 3 + 1, j // 3) if is_peer(k) else (j // 3 + 1, j % 3)
         left = (z + N_Z - dist) % N_Z
         right = (z + dist) % N_Z
-
-        @pl.when(z + dist < N_Z)
-        def _():
-            z_copy(t, k, right, False, False).wait_recv()
-
-            @pl.when(z > 0)
-            def _():
-                z_copy(t, k, right, False, False).start()
-            x_copy(t, k, right).start()
-
-        @pl.when(z >= dist)
-        def _():
-            z_copy(t, k, left, True, False).wait_recv()
-
-            @pl.when(z < N_Z - 1)
-            def _():
-                z_copy(t, k, left, True, False).start()
-            x_copy(t, k, left).start()
+        for u in parts(k, t):
+            @pl.when(z + dist < N_Z)
+            def _():
+                z_copy(u, k, right, False, False).wait_recv()
+
+                @pl.when(z > 0)
+                def _():
+                    z_copy(u, k, right, False, False).start()
+                x_copy(u, k, right).start()
+
+            @pl.when(z >= dist)
+            def _():
+                z_copy(u, k, left, True, False).wait_recv()
+
+                @pl.when(z < N_Z - 1)
+                def _():
+                    z_copy(u, k, left, True, False).start()
+                x_copy(u, k, left).start()
 
         last_packets = isinstance(k, int) and k >= n_packet - 1
         for t in range(3):
@@ -222,7 +233,7 @@
         return pl.ds(pl.multiple_of(shard_at(n) * d_shard, d_shard), d_shard)
 
     def drain(k, own=True, tensors=(0, 1, 2)):
-        for t in tensors:
+        for t in [u for t in tensors for u in parts(k, t)]:
             @pl.when(z > 0)
             def _():
                 z_copy(t, k, z, False, own).wait_send()
@@ -380,20 +391,21 @@
         to_core_near(n).wait_recv()
         cols = columns(n)
         y = toks[3, :, cols].astype(jnp.float32) + (acc[3, :, cols] + from_core[:, cols] + from_y[:, cols])
-        toks[3, :, cols] = y.astype(jnp.bfloat16)
-        copy = pltpu.make_async_copy(toks.at[3, :, cols], out_hbm.at[:, cols], out_sem.at[n])
-        copy.start()
-        return copy
+        out_ref[:, cols] = y.astype(jnp.bfloat16)
+
+    def wait_down(n):
+        for u in parts(n_packet, 2):
+            x_arrival(u, n_packet, shard_at(n)).wait_recv()
 
     outputs(r, 0, False)
+    event(n_packet, N_EVENT - 1)
     outputs(1 - r, 0, True)
     outputs(r, 1, False)
-    event(n_packet, N_EVENT - 1)
-    x_arrival(2, n_packet, shard_at(1)).wait_recv()
+    wait_down(1)
     outputs(1 - r, 1, True)
     outputs(r, 2, False)
     outputs(r, 3, False)
-    x_arrival(2, n_packet, shard_at(2)).wait_recv()
+    wait_down(2)
     outputs(1 - r, 2, True)
     drain(last)
     drain(n_packet, False, (0, 1))
@@ -404,15 +416,15 @@
         to_y(n).wait_recv()
         to_core(n).wait_send()
         to_y(n).wait_send()
-    outs = [finish(n) for n in range(2)]
-    x_arrival(2, n_packet, shard_at(3)).wait_recv()
+    for n in range(2):
+        finish(n)
+    wait_down(3)
     outputs(1 - r, 3, True)
-    outs += [finish(n) for n in range(2, N_Z)]
+    for n in range(2, N_Z):
+        finish(n)
     drain(n_packet, False, (2,))
     for n in range(N_Z):
         to_core_near(n).wait_send()
-    for copy in outs:
-        copy.wait()
 
 
 def solution(mesh):
@@ -428,9 +440,9 @@
         flops = 4 * n_tok * n_local * 6 * d_model * ffn
         return pl.pallas_call(
             moe_kernel,
-            out_shape=jax.ShapeDtypeStruct((n_tok, d_model), jnp.bfloat16),
+            out_shape=pltpu.VMEM((n_tok, d_model), jnp.bfloat16),
             in_specs=[any_space] * 6,
-            out_specs=any_space,
+            out_specs=pl.BlockSpec(memory_space=pltpu.VMEM),
             scratch_shapes=[
                 pltpu.VMEM((n_local, d_model, ffn), jnp.bfloat16),
                 pltpu.VMEM((n_local, d_model, ffn), jnp.bfloat16),
@@ -442,11 +454,11 @@
                 pltpu.VMEM((n_tok, d_model), jnp.float32),
                 pltpu.VMEM((n_tok, d_model), jnp.float32),
                 dma((4, n_local)),
-                dma((3, n_packet + 1, N_Z)),
-                dma((3, n_packet + 1, N_Z)),
-                dma((3, n_packet + 1, N_Z)),
-                dma((3, n_packet + 1, N_Z)),
-                dma((3, n_packet + 1, N_Z)),
+                dma((2 + N_PART, n_packet + 1, N_Z)),
+                dma((2 + N_PART, n_packet + 1, N_Z)),
+                dma((2 + N_PART, n_packet + 1, N_Z)),
+                dma((2 + N_PART, n_packet + 1, N_Z)),
+                dma((2 + N_PART, n_packet + 1, N_Z)),
                 dma((3,)),
                 dma((3,)),
                 dma((2, 3)),
@@ -457,10 +469,9 @@
                 dma((3, N_TAIL)),
                 dma((3, N_TAIL)),
                 pltpu.SemaphoreType.REGULAR((N_TAIL,)),
-                dma((N_TAIL,)),
             ],
             compiler_params=pltpu.CompilerParams(
-                collective_id=0, has_side_effects=True, vmem_limit_bytes=67043328),
+                collective_id=0, has_side_effects=True, vmem_limit_bytes=62914560),
             cost_estimate=pl.CostEstimate(flops=flops, bytes_accessed=32 << 20, transcendentals=0),
             name='moe',
         )(x_blk, ids_blk.T, gate_blk.T, wg_blk, wu_blk, wd_blk)

time: 278 us -> 278 us (level)
  no operation moved by 1% of the time
where the time goes in v6:
time: 278 us
  Pallas kernels  276 us (99%)
    pallas_call x1, Pallas kernels, device_step(): pl.pallas_call(moe_kernel, out_shape=pltpu.VMEM((n_tok, d_model), jnp.bfl...  276 us

profile of v6, /device:TPU:1, one launch (start us, length us, event | category | flops | bytes accessed | tf_op | source)
XLA Modules:
  0.0 277.7 jit_solution(9602377589199479249)
XLA Ops:
  0.0 276.4 %moe.1 = bf16[1024,1024]{1,0:T(8,128)(2,1)S(1)} custom-call(bf16[1024,1024]{1,0:T(8,128)(2,1)} %x_hbm.1, s32[8,1024]{1,0:T(8,128)} %bitcast.2, f32[8,1024]{1,0:T(8,128)} %bitcast.3, bf16[8,256,512]{2,1,0:T(8,128)(2,1)} %wg_hbm.1, bf16[8,256,512]{2,1,0:T(8,128)(2,1)} %wu_hbm.1, bf16[8,512,256]{2,1,0:T(8,128)(2,1)} %wd_hbm.1), custom_call_target="tpu_custom_call" | custom-call | flops 103079215104 | bytes 33554432 | tf_op jit(solution)/shard_map/moe/pallas_call | solution.py:441
  276.4 1.3 copy.8

commit v7 on v6

--- a/solution.py
+++ b/solution.py
@@ -13,10 +13,10 @@
 N_TAIL = 4
 N_EVENT = 9
 LEAD = 2
-N_PART = 4
+N_PART = 1
 STEP_OF = (0, 0, 3, 4, 6, 9, 12, 13, 15)
 STEP_OF_LAST = (2, 5, 6, 6, 8, 11, 12, 15, 17)
-STEP_OF_PEER = (0, 0, 1, 3, 5, 8, 10, 14, 16)
+STEP_OF_PEER = (0, 0, 1, 3, 5, 8, 12, 15, 17)
 OWN_AFTER = (5, 6, 7)
 PEER_OWN_AFTER = (6, 10, 13)
 
@@ -227,7 +227,8 @@
         add_output(h, wd[e, :, pl.ds(start, d_shard)], expert, slot, pl.ds(0, n_tok), start, d_shard)
 
     def shard_at(n):
-        return (z + n + z // 2 * (N_Z - 2 * n)) % N_Z
+        odd, upper = z % 2, z // 2
+        return (z, 1 + odd + 2 * upper - 2 * odd * upper, 2 - 2 * odd - upper + 2 * odd * upper, 3 - 3 * upper)[n]
 
     def columns(n):
         return pl.ds(pl.multiple_of(shard_at(n) * d_shard, d_shard), d_shard)
@@ -365,10 +366,11 @@
         return carry
 
     lax.fori_loop(0, 2 * N_BLOCK, peer_first, 0)
+    event(n_packet, 6)
     wait_x(n_packet, (0, 1))
 
     def peer_second(i, carry):
-        events(i, n_packet, STEP_OF_PEER, LEAD, offset=6 * N_BLOCK)
+        events(i, n_packet, STEP_OF_PEER, 7, offset=6 * N_BLOCK)
         peer_hidden(1 - r, 2 + i // N_BLOCK, i % N_BLOCK)
         return carry
 
@@ -398,9 +400,9 @@
             x_arrival(u, n_packet, shard_at(n)).wait_recv()
 
     outputs(r, 0, False)
-    event(n_packet, N_EVENT - 1)
     outputs(1 - r, 0, True)
     outputs(r, 1, False)
+    event(n_packet, N_EVENT - 1)
     wait_down(1)
     outputs(1 - r, 1, True)
     outputs(r, 2, False)

time: 278 us -> 275 us (0.989)
  Pallas kernels: 276 us -> 273 us
    pallas_call x1, Pallas kernels: 276 us -> 273 us  [device_step(): pl.pallas_call(moe_kernel, out_shape=pltpu.VMEM((n_tok, d_model), jnp.bfl...]
where the time goes in v7:
time: 275 us
  Pallas kernels  273 us (99%)
    pallas_call x1, Pallas kernels, device_step(): pl.pallas_call(moe_kernel, out_shape=pltpu.VMEM((n_tok, d_model), jnp.bfl...  273 us

profile of v7, /device:TPU:1, one launch (start us, length us, event | category | flops | bytes accessed | tf_op | source)
XLA Modules:
  0.0 274.5 jit_solution(3295879659334060925)
XLA Ops:
  0.0 273.2 %moe.1 = bf16[1024,1024]{1,0:T(8,128)(2,1)S(1)} custom-call(bf16[1024,1024]{1,0:T(8,128)(2,1)} %x_hbm.1, s32[8,1024]{1,0:T(8,128)} %bitcast.2, f32[8,1024]{1,0:T(8,128)} %bitcast.3, bf16[8,256,512]{2,1,0:T(8,128)(2,1)} %wg_hbm.1, bf16[8,256,512]{2,1,0:T(8,128)(2,1)} %wu_hbm.1, bf16[8,512,256]{2,1,0:T(8,128)(2,1)} %wd_hbm.1), custom_call_target="tpu_custom_call" | custom-call | flops 103079215104 | bytes 33554432 | tf_op jit(solution)/shard_map/moe/pallas_call | solution.py:443
  273.2 1.3 copy.8

commit v8 on v7

--- a/solution.py
+++ b/solution.py
@@ -13,7 +13,6 @@
 N_TAIL = 4
 N_EVENT = 9
 LEAD = 2
-N_PART = 1
 STEP_OF = (0, 0, 3, 4, 6, 9, 12, 13, 15)
 STEP_OF_LAST = (2, 5, 6, 6, 8, 11, 12, 15, 17)
 STEP_OF_PEER = (0, 0, 1, 3, 5, 8, 12, 15, 17)
@@ -41,20 +40,30 @@
 
     hbm = (wg_hbm, wu_hbm, wd_hbm)
 
-    def shard(t, e, s, k=0):
+    def shard(t, e, s, k):
         start = pl.multiple_of(s * d_shard, d_shard)
-        if is_peer(k) and t >= 2:
-            part = wd.shape[1] // N_PART
-            return wd.at[e, pl.ds((t - 2) * part, part), pl.ds(start, d_shard)]
+        if len(parts(k, 2)) > 1 and t >= 2:
+            half = wd.shape[1] // 2
+            return wd.at[e, pl.ds((t - 2) * half, half), pl.ds(start, d_shard)]
+        if len(parts(k, 0)) > 1 and t in (0, 3):
+            half = d_shard // 2
+            return wg.at[e, pl.ds(pl.multiple_of(start + t // 3 * half, half), half), :]
         if t == 2:
             return wd.at[e, :, pl.ds(start, d_shard)]
         return (wg, wu)[t].at[e, pl.ds(start, d_shard), :]
 
+    def source(t, e, k):
+        if len(parts(k, 0)) > 1 and t in (0, 3):
+            half = d_shard // 2
+            return wg_hbm.at[e, pl.ds(t // 3 * half, half), :]
+        return hbm[t].at[e]
+
     def is_peer(k):
         return isinstance(k, int) and k == n_packet
 
     def parts(k, t):
-        return range(2, 2 + N_PART) if is_peer(k) and t == 2 else (t,)
+        first = isinstance(k, int) and k == 0 and t == 0
+        return (t, 3) if first or (is_peer(k) and t == 2) else (t,)
 
     def remote(src, dst, send_sem, recv_sem, **where):
         return pltpu.make_async_remote_copy(src_ref=src, dst_ref=dst, send_sem=send_sem, recv_sem=recv_sem,
@@ -65,7 +74,7 @@
 
     def z_copy(t, k, s, right, own):
         here = shard(t, place(k) + r, s, k)
-        src = hbm[t].at[place(k) + r] if own else here
+        src = source(t, place(k) + r, k) if own else here
         send = send_r if right else send_l
         to = (z + 1) % N_Z if right else (z + N_Z - 1) % N_Z
         return remote(src, here, send.at[t, k, s], recv_z.at[t, k, s], fsdp=to)
@@ -79,7 +88,7 @@
         return remote(here, here, send_x.at[t, k, s], recv_x.at[t, k, s], rep=1 - r)
 
     def home_copy(t, q):
-        return remote(hbm[t].at[n_local - 2 + q], shard(t, q, z), home_send.at[t, q], home_recv.at[t, q], ep=y_peer)
+        return remote(hbm[t].at[n_local - 2 + q], shard(t, q, z, 1), home_send.at[t, q], home_recv.at[t, q], ep=y_peer)
 
     def send_own(k, t, own=True):
         @pl.when(z > 0)
@@ -139,13 +148,13 @@
 
     def wait_x(k, tensors=(0, 1, 2)):
         for dist in range(1, N_Z):
-            for t in tensors:
+            for t in [u for t in tensors for u in parts(k, t)]:
                 x_arrival(t, k, (z + dist) % N_Z).wait_recv()
 
     barrier = pltpu.get_barrier_semaphore()
     signal_neighbours(barrier, (core_peer, y_peer, far_peer))
 
-    own_w = [pltpu.make_async_copy(hbm[t].at[e], shard(t, e, z), own_sem.at[t, e])
+    own_w = [pltpu.make_async_copy(hbm[t].at[e], shard(t, e, z, 1), own_sem.at[t, e])
              for e in range(n_local) for t in range(3)]
     own_x = pltpu.make_async_copy(x_hbm, toks.at[3], own_sem.at[3, 0])
     own_ids = pltpu.make_async_copy(ids_hbm, ids.at[3], own_sem.at[3, 1])
@@ -157,14 +166,14 @@
     z_peers = (z + N_Z - 1) // N_Z + (2 * N_Z - 2 - z) // N_Z
     pl.semaphore_wait(barrier, 4 + z_peers)
 
+    for t in range(3):
+        send_own(0, t)
     meta = []
     for slot, peer in ((2, core_peer), (1, y_peer), (0, far_peer)):
         meta.append(remote(ids_hbm, ids.at[slot], meta_send.at[0, slot], meta_recv.at[0, slot], ep=peer))
         meta.append(remote(gates_hbm, gates.at[slot], meta_send.at[1, slot], meta_recv.at[1, slot], ep=peer))
     for copy in meta:
         copy.start()
-    for t in range(3):
-        send_own(0, t)
     tok_core = remote(x_hbm, toks.at[2], tok_send.at[2], tok_recv.at[2], ep=core_peer)
     tok_y = remote(x_hbm, toks.at[1], tok_send.at[1], tok_recv.at[1], ep=y_peer)
     tok_far = remote(toks.at[1], toks.at[0], tok_send.at[0], tok_recv.at[0], ep=core_peer)
@@ -409,6 +418,8 @@
     outputs(r, 3, False)
     wait_down(2)
     outputs(1 - r, 2, True)
+    wait_down(3)
+    outputs(1 - r, 3, True)
     drain(last)
     drain(n_packet, False, (0, 1))
     for t in range(3):
@@ -418,11 +429,7 @@
         to_y(n).wait_recv()
         to_core(n).wait_send()
         to_y(n).wait_send()
-    for n in range(2):
-        finish(n)
-    wait_down(3)
-    outputs(1 - r, 3, True)
-    for n in range(2, N_Z):
+    for n in range(N_Z):
         finish(n)
     drain(n_packet, False, (2,))
     for n in range(N_Z):
@@ -456,11 +463,11 @@
                 pltpu.VMEM((n_tok, d_model), jnp.float32),
                 pltpu.VMEM((n_tok, d_model), jnp.float32),
                 dma((4, n_local)),
-                dma((2 + N_PART, n_packet + 1, N_Z)),
-                dma((2 + N_PART, n_packet + 1, N_Z)),
-                dma((2 + N_PART, n_packet + 1, N_Z)),
-                dma((2 + N_PART, n_packet + 1, N_Z)),
-                dma((2 + N_PART, n_packet + 1, N_Z)),
+                dma((4, n_packet + 1, N_Z)),
+                dma((4, n_packet + 1, N_Z)),
+                dma((4, n_packet + 1, N_Z)),
+                dma((4, n_packet + 1, N_Z)),
+                dma((4, n_packet + 1, N_Z)),
                 dma((3,)),
                 dma((3,)),
                 dma((2, 3)),

time: 275 us -> 276 us (level)
  no operation moved by 1% of the time
where the time goes in v8:
time: 276 us; the launch traced here: 275 us
  Pallas kernels  274 us (99%)
    pallas_call x1, Pallas kernels, device_step(): pl.pallas_call(moe_kernel, out_shape=pltpu.VMEM((n_tok, d_model), jnp.bfl...  274 us

profile of v8, /device:TPU:1, one launch (start us, length us, event | category | flops | bytes accessed | tf_op | source)
XLA Modules:
  0.0 275.4 jit_solution(4379271435503731166)
XLA Ops:
  0.0 274.1 %moe.1 = bf16[1024,1024]{1,0:T(8,128)(2,1)S(1)} custom-call(bf16[1024,1024]{1,0:T(8,128)(2,1)} %x_hbm.1, s32[8,1024]{1,0:T(8,128)} %bitcast.2, f32[8,1024]{1,0:T(8,128)} %bitcast.3, bf16[8,256,512]{2,1,0:T(8,128)(2,1)} %wg_hbm.1, bf16[8,256,512]{2,1,0:T(8,128)(2,1)} %wu_hbm.1, bf16[8,512,256]{2,1,0:T(8,128)(2,1)} %wd_hbm.1), custom_call_target="tpu_custom_call" | custom-call | flops 103079215104 | bytes 33554432 | tf_op jit(solution)/shard_map/moe/pallas_call | solution.py:450
  274.1 1.3 copy.8

commit v9 on v7

--- a/solution.py
+++ b/solution.py
@@ -157,14 +157,14 @@
     z_peers = (z + N_Z - 1) // N_Z + (2 * N_Z - 2 - z) // N_Z
     pl.semaphore_wait(barrier, 4 + z_peers)
 
+    for t in range(3):
+        send_own(0, t)
     meta = []
     for slot, peer in ((2, core_peer), (1, y_peer), (0, far_peer)):
         meta.append(remote(ids_hbm, ids.at[slot], meta_send.at[0, slot], meta_recv.at[0, slot], ep=peer))
         meta.append(remote(gates_hbm, gates.at[slot], meta_send.at[1, slot], meta_recv.at[1, slot], ep=peer))
     for copy in meta:
         copy.start()
-    for t in range(3):
-        send_own(0, t)
     tok_core = remote(x_hbm, toks.at[2], tok_send.at[2], tok_recv.at[2], ep=core_peer)
     tok_y = remote(x_hbm, toks.at[1], tok_send.at[1], tok_recv.at[1], ep=y_peer)
     tok_far = remote(toks.at[1], toks.at[0], tok_send.at[0], tok_recv.at[0], ep=core_peer)
@@ -409,6 +409,8 @@
     outputs(r, 3, False)
     wait_down(2)
     outputs(1 - r, 2, True)
+    wait_down(3)
+    outputs(1 - r, 3, True)
     drain(last)
     drain(n_packet, False, (0, 1))
     for t in range(3):
@@ -418,11 +420,7 @@
         to_y(n).wait_recv()
         to_core(n).wait_send()
         to_y(n).wait_send()
-    for n in range(2):
-        finish(n)
-    wait_down(3)
-    outputs(1 - r, 3, True)
-    for n in range(2, N_Z):
+    for n in range(N_Z):
         finish(n)
     drain(n_packet, False, (2,))
     for n in range(N_Z):

time: 275 us -> 275 us (level)
  no operation moved by 1% of the time
where the time goes in v9:
time: 275 us
  Pallas kernels  273 us (99%)
    pallas_call x1, Pallas kernels, device_step(): pl.pallas_call(moe_kernel, out_shape=pltpu.VMEM((n_tok, d_model), jnp.bfl...  273 us

profile of v9, /device:TPU:1, one launch (start us, length us, event | category | flops | bytes accessed | tf_op | source)
XLA Modules:
  0.0 274.5 jit_solution(15982558771762699072)
XLA Ops:
  0.0 273.2 %moe.1 = bf16[1024,1024]{1,0:T(8,128)(2,1)S(1)} custom-call(bf16[1024,1024]{1,0:T(8,128)(2,1)} %x_hbm.1, s32[8,1024]{1,0:T(8,128)} %bitcast.2, f32[8,1024]{1,0:T(8,128)} %bitcast.3, bf16[8,256,512]{2,1,0:T(8,128)(2,1)} %wg_hbm.1, bf16[8,256,512]{2,1,0:T(8,128)(2,1)} %wu_hbm.1, bf16[8,512,256]{2,1,0:T(8,128)(2,1)} %wd_hbm.1), custom_call_target="tpu_custom_call" | custom-call | flops 103079215104 | bytes 33554432 | tf_op jit(solution)/shard_map/moe/pallas_call | solution.py:441
  273.2 1.3 copy.8
